TPU v7x, 512 devices: a whole 4x4x16 slice. The times are simulated.
512 devices in a mesh: prow: 32 (over z, y_hi), pcol: 16 (over y_lo, x, core).
Axes of the slice: x: 4, y: 4 (y_hi: 2, y_lo: 2; y = y_hi * 2 + y_lo), z: 16, core: 2. Of those that a mesh axis runs over, the one named last changes fastest.
Arguments:
- matrix: float32 [8192, 8192], P('prow', 'pcol'), as said below
Outputs:
- complement: float32 [8192, 8192], P('prow', 'pcol')
- panel_columns: float32 [8192, 512], P(('prow', 'pcol'))
- pivot_values: float32 [512], replicated
Inputs may be any that keep to these rules, and one draw needn't show every extreme that they name: matrix is symmetric and positive definite, with its smallest eigenvalue above a six-hundredth of its largest diagonal entry.
All inputs are finite; a program needn't handle non-finite values.
Results may differ from a plain program's by a relative error of at most 0.00014.
Values sent between devices are 32-bit elements; how exact they have to be, the bound alone decides.
No kernel may reach another device: no remote copies, remote signals or barrier semaphores. Data moves between devices by JAX's collectives and lax.ppermute only.
A program may use at most 128 MiB of HBM per device.

v0:
```python
import jax
import jax.numpy as jnp
from jax import lax
from jax.sharding import Mesh
from jax.sharding import PartitionSpec as P

NB = 256
PANELS = 2
PROW = ("prow_0", "prow_1")
PROW_PCOL = ("prow_0", "prow_1", "pcol")


HIGHEST = lax.Precision.HIGHEST


def from_root(array, axes, root):
    array = jnp.where(lax.axis_index(axes) == root, array, jnp.zeros_like(array))
    for axis in axes:
        array = lax.psum(array, axis)
    return array


def picked(array, axis, root):
    return lax.dynamic_index_in_dim(lax.all_gather(array, axis), root, 0, keepdims=False)


def factor_diagonal(diagonal):
    cholesky_factor = jnp.linalg.cholesky(diagonal)
    scaling = jnp.diagonal(cholesky_factor)
    identity = jnp.eye(diagonal.shape[0], dtype=diagonal.dtype)
    inverse = jax.scipy.linalg.solve_triangular(cholesky_factor, identity, lower=True)
    return (inverse, scaling)


def against(left_side, right_side):
    return lax.dot_general(left_side, right_side, (((1,), (1,)), ((), ())), precision=HIGHEST)


def refreshed(current, weighed, partner, finished, row_base, col_base, bounds):
    row_start, row_stop, col_start, col_stop = bounds
    section = current - against(weighed, partner)
    extent = section.shape
    global_rows = row_base + row_start + lax.broadcasted_iota(jnp.int32, extent, 0)
    global_cols = col_base + col_start + lax.broadcasted_iota(jnp.int32, extent, 1)
    retained = (global_rows >= finished) & (global_cols >= finished)
    return jnp.where(retained, section, jnp.zeros_like(section))


def on_device(matrix):
    current = matrix
    row_count, col_count = matrix.shape
    col_groups = lax.axis_size("pcol")
    row_base = lax.axis_index(PROW) * row_count
    col_base = lax.axis_index("pcol") * col_count
    portion = row_count // col_groups
    column_list = []
    pivot_list = []
    for panel in range(PANELS):
        first = panel * NB
        root_row = first // row_count
        row_offset = first % row_count
        root_col = first // col_count
        col_offset = first % col_count
        row_strip = current
        received = from_root(row_strip, PROW, root_row)
        inverse, scaling = factor_diagonal(received[:, col_offset : col_offset + NB])
        projected = against(current[:, col_offset : col_offset + NB], inverse)
        factored, inverse, scaling = (
            picked(projected * scaling, "pcol", root_col),
            picked(inverse, "pcol", root_col),
            picked(scaling, "pcol", root_col),
        )
        partner = (
            lax.dot_general(received, inverse, (((0,), (1,)), ((), ())), precision=HIGHEST)
            * scaling
        )
        pivot = scaling * scaling
        weighed = factored / pivot
        finished = first + NB
        bounds_list = [(0, row_count, 0, col_count)]
        joined_axis = 1
        sections = [
            refreshed(current, weighed, partner, finished, row_base, col_base, bounds)
            for bounds in bounds_list
        ]
        current = sections[0]
        column_list.append(
            lax.dynamic_slice_in_dim(factored, lax.axis_index("pcol") * portion, portion, 0)
        )
        pivot_list.append(pivot)
    return (current, jnp.concatenate(column_list, axis=1), jnp.concatenate(pivot_list))


def solution(mesh):
    split = Mesh(mesh.devices.reshape(16, 2, mesh.shape["pcol"]), ("prow_0", "prow_1", "pcol"))
    in_specs = (P(PROW, "pcol"),)
    out_specs = (P(PROW, "pcol"), P(PROW_PCOL, None), P())
    return jax.shard_map(
        on_device, mesh=split, in_specs=in_specs, out_specs=out_specs, check_vma=False
    )
```

profile of v0, /device:TPU:1, one launch (start us, length us, event | category | flops | bytes accessed | tf_op | source)
XLA Modules:
  0.0 724.1 jit_solution(15212557457940428483)
XLA Ops:
  7.2 1.2 copy.24
  9.4 134.9 %all-reduce.6.cloned.1.call-done = f32[256,512]{0,1:T(8,128)} async-done(((f32[256,512]{0,1:T(8,128)}), f32[256,512]{0,1:T(8,128)}) %all-reduce.6.cloned.1.call-update) | async-done | bytes 524304 | tf_op jit(solution)/shard_map/psum | solution.py:19
  144.4 61.1 %all-reduce.8.cloned.1.call-done = f32[256,512]{0,1:T(8,128)} async-done(((f32[256,512]{0,1:T(8,128)}), f32[256,512]{0,1:T(8,128)}) %all-reduce.8.cloned.1.call-update) | async-done | bytes 524304 | tf_op jit(solution)/shard_map/psum | solution.py:19
  207.7 11.7 %cholesky.130 = f32[128,128]{1,0:T(8,128)S(1)} custom-call(f32[128,128]{1,0:T(8,128)S(1)} %cholesky.194), custom_call_target="Cholesky" | custom-call | tf_op jit(solution)/shard_map/jit(cholesky)/cholesky | solution.py:28
  219.4 9.8 %custom-call.17 = f32[1,128,128]{1,2,0:T(8,128)S(1)} custom-call(f32[1,128,128]{2,1,0:T(8,128)S(1)} %get-tuple-element.61), custom_call_target="InvertDiagBlocksLowerTriangular" | custom-call | tf_op jit(solution)/shard_map/jit(cholesky)/cholesky | solution.py:28
  229.8 11.7 %cholesky.147 = f32[128,128]{1,0:T(8,128)S(1)} custom-call(f32[128,128]{1,0:T(8,128)S(1)} %convolution_subtract_fusion.5), custom_call_target="Cholesky" | custom-call | tf_op jit(solution)/shard_map/jit(cholesky)/cholesky | solution.py:28
  243.6 4.2 while.4
  244.4 1.4 bitcast_dynamic-update-slice_fusion.4
  246.4 1.4 bitcast_dynamic-update-slice_fusion.4
  247.8 19.7 %custom-call.18 = f32[2,128,128]{1,2,0:T(8,128)S(1)} custom-call(f32[2,128,128]{2,1,0:T(8,128)S(1)} %get-tuple-element.19), custom_call_target="InvertDiagBlocksLowerTriangular" | custom-call | tf_op jit(solution)/shard_map/jit(_solve_triangular)/triangular_solve | solution.py:31
  269.2 2.3 gather_fusion
  272.8 19.3 %all-gather.6 = f32[16,1,256]{2,1,0:T(1,128)S(1)} all-gather(f32[1,1,256]{2,1,0:T(1,128)S(1)} %bitcast.82), channel_id=3, replica_groups=mesh['prow_0'=16,'prow_1'=2,'pcol'=16] {'pcol'}, dimensions={0}, use_global_device_ids=true | all-gather | bytes 17408 | tf_op jit(solution)/shard_map/all_gather | solution.py:24
  292.1 22.0 %all-gather.15.cloned.1.call-done = f32[4096,256]{1,0:T(8,128)} async-done(((f32[256,256]{1,0:T(8,128)}), f32[4096,256]{1,0:T(8,128)}) %all-gather.15.cloned.1.call-update) | async-done | bytes 4194320 | tf_op jit(solution)/shard_map/all_gather | solution.py:24
  314.1 1.6 convolution_multiply_fusion.1
  315.7 45.4 %all-gather.13.cloned.1.call-done = f32[4096,256]{0,1:T(8,128)} async-done(((f32[256,256]{0,1:T(8,128)}), f32[4096,256]{0,1:T(8,128)}) %all-gather.13.cloned.1.call-update) | async-done | bytes 4194320 | tf_op jit(solution)/shard_map/all_gather | solution.py:24
  361.0 2.4 broadcast_select_fusion
  363.5 128.0 %all-reduce.10.cloned.1.call-done = f32[256,512]{0,1:T(8,128)} async-done(((f32[256,512]{0,1:T(8,128)}), f32[256,512]{0,1:T(8,128)}) %all-reduce.10.cloned.1.call-update) | async-done | bytes 524304 | tf_op jit(solution)/shard_map/psum | solution.py:19
  491.6 61.0 %all-reduce.12.cloned.1.call-done = f32[256,512]{0,1:T(8,128)} async-done(((f32[256,512]{0,1:T(8,128)}), f32[256,512]{0,1:T(8,128)}) %all-reduce.12.cloned.1.call-update) | async-done | bytes 524304 | tf_op jit(solution)/shard_map/psum | solution.py:19
  554.8 11.7 %cholesky.164 = f32[128,128]{1,0:T(8,128)S(1)} custom-call(f32[128,128]{1,0:T(8,128)S(1)} %cholesky.197), custom_call_target="Cholesky" | custom-call | tf_op jit(solution)/shard_map/jit(cholesky)/cholesky | solution.py:28
  567.2 9.8 %custom-call.19 = f32[1,128,128]{1,2,0:T(8,128)S(1)} custom-call(f32[1,128,128]{2,1,0:T(8,128)S(1)} %get-tuple-element.57), custom_call_target="InvertDiagBlocksLowerTriangular" | custom-call | tf_op jit(solution)/shard_map/jit(cholesky)/cholesky | solution.py:28
  577.5 11.7 %cholesky.181 = f32[128,128]{1,0:T(8,128)S(1)} custom-call(f32[128,128]{1,0:T(8,128)S(1)} %convolution_subtract_fusion.4), custom_call_target="Cholesky" | custom-call | tf_op jit(solution)/shard_map/jit(cholesky)/cholesky | solution.py:28
  591.3 2.6 gather_fusion.1
  593.9 4.0 while.5
  594.5 1.4 bitcast_dynamic-update-slice_fusion.5
  596.5 1.4 bitcast_dynamic-update-slice_fusion.5
  597.9 19.7 %custom-call.20 = f32[2,128,128]{1,2,0:T(8,128)S(1)} custom-call(f32[2,128,128]{2,1,0:T(8,128)S(1)} %get-tuple-element.20), custom_call_target="InvertDiagBlocksLowerTriangular" | custom-call | tf_op jit(solution)/shard_map/jit(_solve_triangular)/triangular_solve | solution.py:31
  618.5 1.3 convolution_multiply_fusion.2
  620.8 19.3 %all-gather.7 = f32[16,1,256]{2,1,0:T(1,128)S(1)} all-gather(f32[1,1,256]{2,1,0:T(1,128)S(1)} %bitcast.81), channel_id=6, replica_groups=mesh['prow_0'=16,'prow_1'=2,'pcol'=16] {'pcol'}, dimensions={0}, use_global_device_ids=true | all-gather | bytes 17408 | tf_op jit(solution)/shard_map/all_gather | solution.py:24
  640.7 24.0 %all-gather.17.cloned.1.call-done = f32[4096,256]{1,0:T(8,128)} async-done(((f32[256,256]{1,0:T(8,128)}), f32[4096,256]{1,0:T(8,128)}) %all-gather.17.cloned.1.call-update) | async-done | bytes 4194320 | tf_op jit(solution)/shard_map/all_gather | solution.py:24
  665.8 46.7 %all-gather.19.cloned.1.call-done = f32[4096,256]{1,0:T(8,128)} async-done(((f32[256,256]{1,0:T(8,128)}), f32[4096,256]{1,0:T(8,128)}) %all-gather.19.cloned.1.call-update) | async-done | bytes 4194320 | tf_op jit(solution)/shard_map/all_gather | solution.py:24
  712.5 1.6 convolution_multiply_fusion
  714.1 1.6 fusion
  (86 shorter events, 18.9 us)
Async XLA Ops:
  7.2 137.1 %all-reduce.6.cloned.1.call-start = ((), (), s32[]{:S(2)}) async-start(), calls=%async_computation | async-start | bytes 1048576 | tf_op jit(solution)/shard_map/psum | solution.py:19
  9.3 196.2 %all-reduce.8.cloned.1.call-start = ((), (), s32[]{:S(2)}) async-start(), calls=%async_computation.1 | async-start | bytes 1048576 | tf_op jit(solution)/shard_map/psum | solution.py:19
  144.3 127.2 %copy-start.2 = (f32[256,512]{1,0:T(8,128)S(1)}, f32[256,512]{1,0:T(8,128)}, u32[]{:S(2)}) copy-start(f32[256,512]{1,0:T(8,128)} %param.4) | copy-start | bytes 1572868
  144.3 169.8 %all-gather.15.cloned.1.call-start = ((), (), s32[]{:S(2)}) async-start(), calls=%async_computation.5 | async-start | bytes 4456448 | tf_op jit(solution)/shard_map/all_gather | solution.py:24
  206.5 107.6 %copy-start.1 = (f32[256,512]{0,1:T(8,128)S(1)}, f32[256,512]{0,1:T(8,128)}, u32[]{:S(2)}) copy-start(f32[256,512]{0,1:T(8,128)} %all-reduce.8.cloned.1.call-done) | copy-start | bytes 1572868
  269.1 91.9 %all-gather.13.cloned.1.call-start = ((), (), s32[]{:S(2)}) async-start(), calls=%async_computation.4 | async-start | bytes 4456448 | tf_op jit(solution)/shard_map/all_gather | solution.py:24
  272.7 218.9 %all-reduce.10.cloned.1.call-start = ((), (), s32[]{:S(2)}) async-start(), calls=%async_computation.2 | async-start | bytes 1048576 | tf_op jit(solution)/shard_map/psum | solution.py:19
  363.5 189.2 %all-reduce.12.cloned.1.call-start = ((), (), s32[]{:S(2)}) async-start(), calls=%async_computation.3 | async-start | bytes 1048576 | tf_op jit(solution)/shard_map/psum | solution.py:19
  491.6 173.2 %all-gather.17.cloned.1.call-start = ((), (), s32[]{:S(2)}) async-start(), calls=%async_computation.6 | async-start | bytes 4456448 | tf_op jit(solution)/shard_map/all_gather | solution.py:24
  553.8 66.9 %slice-start = ((f32[4096,256]{0,1:T(8,128)}), f32[256,256]{0,1:T(8,128)S(1)}, s32[]{:S(2)}) async-start(f32[4096,256]{0,1:T(8,128)} %all-gather.13.cloned.1.call-done), calls=%async_computation.8 | async-start | bytes 524288 | tf_op jit(solution)/shard_map/jit(dynamic_index_in_dim)/dynamic_slice | solution.py:24
  577.0 135.5 %copy-start = (f32[256,512]{0,1:T(8,128)S(1)}, f32[256,512]{0,1:T(8,128)}, u32[]{:S(2)}) copy-start(f32[256,512]{0,1:T(8,128)} %all-reduce.12.cloned.1.call-done) | copy-start | bytes 1572868
  619.8 92.7 %all-gather.19.cloned.1.call-start = ((), (), s32[]{:S(2)}) async-start(), calls=%async_computation.7 | async-start | bytes 4456448 | tf_op jit(solution)/shard_map/all_gather | solution.py:24
Sparse Core Ops, SparseCore 0:
  10.9 133.3 all-reduce.5
  147.2 58.3 all-reduce.7
  269.2 44.8 all-gather.14
  316.0 44.9 all-gather.12
  363.8 127.7 all-reduce.9
  494.3 58.3 all-reduce.11
  619.9 44.7 all-gather.16
  667.5 44.9 all-gather.18
where the time goes:
time: 725 us; the launch traced here: 724 us
  waiting for transfers between devices  523 us (72%)
  other arithmetic  114 us (16%)
  blocking collectives  38.7 us (5%)
  local copies, waits for them, and re-layouts  18.5 us (3%)
  between operations  17.1 us (2%)
  matrix products  12.3 us (2%)
    psum x4, waiting for transfers between devices, from_root(): array = lax.psum(array, axis)  385 us
    all_gather x4, waiting for transfers between devices, picked(): lax.all_gather(array, axis)  138 us
    another operation x13, other arithmetic, factor_diagonal(): cholesky_factor = jnp.linalg.cholesky(diagonal)  68.5 us
    another operation x7, other arithmetic, factor_diagonal(): jax.scipy.linalg.solve_triangular(cholesky_factor, identity, lower=True)  40.9 us
    all_gather x2, blocking collectives, picked(): lax.all_gather(array, axis)  38.7 us
  transfers between devices with their start and end apart: 8, of which 8 were waited for; matrix products, arithmetic and copies ran while one was open for 1% of the time, Pallas kernels for 0%

commit v1 on v0

v1 whole, which is shorter than its diff:
```python
import jax
import jax.numpy as jnp
from jax import lax
from jax.experimental import pallas as pl
from jax.experimental.pallas import tpu as pltpu
from jax.sharding import Mesh
from jax.sharding import PartitionSpec as P

NB = 256
PANELS = 2
WIDTH = NB * PANELS
BLOCK = 128
STEP = 8
PROW = ("z", "yh")
HIGHEST = lax.Precision.HIGHEST


def product(left, right, left_axis, right_axis):
    return lax.dot_general(
        left,
        right,
        (((left_axis,), (right_axis,)), ((), ())),
        precision=HIGHEST,
        preferred_element_type=jnp.float32,
    )


def factor_block(work, inverse, scaled, base):
    sublane = lax.broadcasted_iota(jnp.int32, (STEP, BLOCK), 0)

    def spread_row(value, index):
        return jnp.broadcast_to(value[index : index + 1, :], (STEP, BLOCK))

    def spread_column(value, index):
        return jnp.broadcast_to(value[:, index : index + 1], (STEP, BLOCK))

    steps = BLOCK // STEP
    for step in range(steps):
        at = STEP * step
        ahead = step < steps - 1
        rows = work[base + at : base + at + STEP, base : base + BLOCK]
        turned = inverse[at : at + STEP, :]
        columns = [spread_column(rows, at + j) for j in range(STEP)]
        if ahead:
            next_rows = work[base + at + STEP : base + at + 2 * STEP, base : base + BLOCK]
            next_turned = inverse[at + STEP : at + 2 * STEP, :]
            next_columns = [spread_column(next_rows, at + j) for j in range(STEP)]
        reciprocals = jnp.zeros((STEP, BLOCK), jnp.float32)
        for k in range(STEP):
            reciprocal = 1.0 / spread_row(columns[k], k)
            factor = jnp.where(sublane > k, columns[k] * reciprocal, 0.0)
            if ahead:
                next_factor = next_columns[k] * reciprocal
            for j in range(k + 1, STEP):
                pivot_entry = spread_row(columns[j], k)
                columns[j] = columns[j] - factor * pivot_entry
                if ahead:
                    next_columns[j] = next_columns[j] - next_factor * pivot_entry
            pivot_row = spread_row(rows, k)
            pivot_turned = spread_row(turned, k)
            rows = rows - factor * pivot_row
            turned = turned - factor * pivot_turned
            if ahead:
                next_rows = next_rows - next_factor * pivot_row
                next_turned = next_turned - next_factor * pivot_turned
            reciprocals = jnp.where(sublane == k, reciprocal, reciprocals)
        work[base + at : base + at + STEP, base : base + BLOCK] = rows
        inverse[at : at + STEP, :] = turned
        scaled[at : at + STEP, :] = turned * reciprocals
        if ahead:
            work[base + at + STEP : base + at + 2 * STEP, base : base + BLOCK] = next_rows
            inverse[at + STEP : at + 2 * STEP, :] = next_turned
        if step < steps - 2:
            later = at + 2 * STEP
            change = product(rows * reciprocals, jnp.concatenate([rows, turned], axis=1), 0, 0)
            work[base + later : base + BLOCK, base : base + BLOCK] = (
                work[base + later : base + BLOCK, base : base + BLOCK] - change[later:, :BLOCK]
            )
            inverse[later:, :] = inverse[later:, :] - change[later:, BLOCK:]


def factor_kernel(place, gathered, other, inverse, pivots, work, block_inverse, block_scaled):
    own = gathered[:, 16:32, :].reshape(NB, WIDTH)

    @pl.when(place[0] == 0)
    def _():
        work[:NB, :] = own
        work[NB:, :NB] = own[:, NB:].T
        work[NB:, NB:] = other[...]

    @pl.when(place[0] == 1)
    def _():
        work[NB:, :] = own
        work[:NB, NB:] = own[:, :NB].T
        work[:NB, :NB] = other[...]

    inverse[...] = jnp.zeros((WIDTH, WIDTH), jnp.float32)
    diagonal = lax.broadcasted_iota(jnp.int32, (BLOCK, BLOCK), 0) == lax.broadcasted_iota(
        jnp.int32, (BLOCK, BLOCK), 1
    )
    for base in range(0, WIDTH, BLOCK):
        end = base + BLOCK
        block_inverse[...] = diagonal.astype(jnp.float32)
        factor_block(work, block_inverse, block_scaled, base)
        pivots[:, base:end] = jnp.sum(
            jnp.where(diagonal, work[base:end, base:end], 0.0), axis=0, keepdims=True
        )
        if end < WIDTH:
            right = product(block_scaled[...], work[base:end, end:], 1, 0)
            left = product(work[end:, base:end], block_inverse[...], 1, 1)
            work[end:, end:] = work[end:, end:] - product(left, right, 1, 0)
        if base > 0:
            scaled_rows = product(block_scaled[...], inverse[base:end, :base], 1, 0)
            inverse[base:end, :base] = product(
                block_inverse[...], inverse[base:end, :base], 1, 0
            )
        inverse[base:end, base:end] = block_inverse[...]
        if end < WIDTH:
            if base > 0:
                inverse[end:, :base] = inverse[end:, :base] - product(left, scaled_rows, 1, 0)
            inverse[end:, base:end] = inverse[end:, base:end] - product(
                left, block_scaled[...], 1, 0
            )


def apply_kernel(place, matrix, gathered, other, inverse, pivots, complement, panel, scratch):
    half, row_block, col_block = place[0], place[1], place[2]
    factored = product(gathered[:, 32:48, :].reshape(NB, WIDTH), inverse[...], 1, 1)
    lane = lax.broadcasted_iota(jnp.int32, (NB, WIDTH), 1)
    scratch[...] = jnp.where((row_block == 0) & (lane >= NB), 0.0, factored)
    panel[...] = scratch[pl.ds(pl.multiple_of(16 * col_block, 16), 16), :]
    weighed = product(factored / pivots[...], inverse[...], 1, 0)
    kept = (row_block >= PANELS) & (col_block >= 1)
    first = pl.ds(pl.multiple_of(NB * half, NB), NB)
    second = pl.ds(pl.multiple_of(NB * (1 - half), NB), NB)
    change = product(weighed, gathered[:, :16, :].reshape(NB, WIDTH), 1, 1)
    complement[:, first] = jnp.where(kept, matrix[:, first] - change, 0.0)
    change = product(weighed, other[...], 1, 1)
    complement[:, second] = jnp.where(kept, matrix[:, second] - change, 0.0)


def on_device(matrix):
    half = lax.axis_index("yh")
    row_block = lax.axis_index(PROW)
    col_block = lax.axis_index("pcol")
    place = jnp.stack([half, row_block, col_block]).astype(jnp.int32)
    columns = lax.axis_size("pcol")
    scattered = lax.all_to_all(
        matrix.reshape(columns, -1, WIDTH), "pcol", 0, 0, tiled=True
    )[0]
    along = lax.all_gather(scattered, "z")
    packed = jnp.concatenate(
        [
            along,
            jnp.broadcast_to(along[:1], along.shape),
            jnp.broadcast_to(scattered[None], along.shape),
        ],
        axis=1,
    )
    gathered = lax.all_to_all(packed, "pcol", 0, 0, tiled=True)
    swap = [(0, 1), (1, 0)]
    corner = lax.dynamic_slice_in_dim(
        gathered[:, 16:32, :].reshape(NB, WIDTH), half * NB, NB, axis=1
    )
    other_corner = lax.ppermute(corner, "yh", swap)
    columns_half, other_corner = lax.optimization_barrier(
        (gathered[:, :16, :].reshape(NB, WIDTH), other_corner)
    )
    other_columns = lax.ppermute(columns_half, "yh", swap)
    smem = pl.BlockSpec(memory_space=pltpu.SMEM)
    vmem = pl.BlockSpec(memory_space=pltpu.VMEM)
    inverse, pivots = pl.pallas_call(
        factor_kernel,
        out_shape=(
            jax.ShapeDtypeStruct((WIDTH, WIDTH), jnp.float32),
            jax.ShapeDtypeStruct((1, WIDTH), jnp.float32),
        ),
        in_specs=[smem, vmem, vmem],
        out_specs=(vmem, vmem),
        scratch_shapes=[
            pltpu.VMEM((WIDTH, WIDTH), jnp.float32),
            pltpu.VMEM((BLOCK, BLOCK), jnp.float32),
            pltpu.VMEM((BLOCK, BLOCK), jnp.float32),
        ],
        cost_estimate=pl.CostEstimate(
            flops=200_000_000, bytes_accessed=3_000_000, transcendentals=0
        ),
        name="factor",
    )(place, gathered, other_corner)
    complement, panel = pl.pallas_call(
        apply_kernel,
        out_shape=(
            jax.ShapeDtypeStruct(matrix.shape, jnp.float32),
            jax.ShapeDtypeStruct((16, WIDTH), jnp.float32),
        ),
        in_specs=[smem, vmem, vmem, vmem, vmem, vmem],
        out_specs=(vmem, vmem),
        scratch_shapes=[pltpu.VMEM((NB, WIDTH), jnp.float32)],
        cost_estimate=pl.CostEstimate(
            flops=400_000_000, bytes_accessed=5_000_000, transcendentals=0
        ),
        name="apply",
    )(place, matrix, gathered, other_columns, inverse, pivots)
    return complement, panel, pivots.reshape(WIDTH)


def solution(mesh):
    split = Mesh(mesh.devices.reshape(16, 2, mesh.shape["pcol"]), ("z", "yh", "pcol"))
    return jax.shard_map(
        on_device,
        mesh=split,
        in_specs=(P(PROW, "pcol"),),
        out_specs=(P(PROW, "pcol"), P((*PROW, "pcol"), None), P()),
        check_vma=False,
    )
```

time: 725 us -> 133 us (0.18)
  waiting for transfers between devices: 523 us -> 27.4 us
  other arithmetic: 114 us -> 1.91 us
  Pallas kernels: 0 us -> 33.1 us
  starting transfers between devices: 0.32 us -> 21.1 us
  local copies, waits for them, and re-layouts: 18.5 us -> 1.03 us
  between operations: 17.1 us -> 0.7 us
  matrix products: 12.3 us -> 0 us
  blocking collectives: 38.7 us -> 47.6 us
    psum x4 -> x0, waiting for transfers between devices: 385 us -> none  [from_root(): array = lax.psum(array, axis)]
    all_gather x4 -> x0, waiting for transfers between devices: 138 us -> none  [picked(): lax.all_gather(array, axis)]
    another operation x20 -> x1, other arithmetic: 109 us -> 0.58 us  [on_device(): place = jnp.stack([half, row_block, col_block]).astype(jnp.int32)]
    pallas_call x0 -> x2, Pallas kernels: none -> 33.1 us  [the longest x1 27.4 us: on_device(): pl.pallas_call(factor_kernel, out_shape=(jax.ShapeDtypeStruct((WIDTH, WID...]
    all_to_all x0 -> x1, waiting for transfers between devices: none -> 21.5 us  [on_device(): gathered = lax.all_to_all(packed, 'pcol', 0, 0, tiled=True)]
    all_to_all x0 -> x1, blocking collectives: none -> 19.8 us  [on_device(): lax.all_to_all(matrix.reshape(columns, -1, WIDTH), 'pcol', 0, 0, tiled=True)]
    all_to_all x0 -> x1, starting transfers between devices: none -> 12.1 us  [on_device(): gathered = lax.all_to_all(packed, 'pcol', 0, 0, tiled=True)]
    all_gather x2 -> x1, blocking collectives: 38.7 us -> 27.8 us  [on_device(): along = lax.all_gather(scattered, 'z')]
  transfers between devices with their start and end apart: 8 -> 3, of which waited for: 8 -> 2; matrix products, arithmetic and copies ran while one was open for 1% -> 0% of each run, Pallas kernels for 0% -> 21%
where the time goes in v1:
time: 133 us
  blocking collectives  47.6 us (36%)
  Pallas kernels  33.1 us (25%)
  waiting for transfers between devices  27.4 us (21%)
  starting transfers between devices  21.1 us (16%)
  other arithmetic  1.91 us (1%)
    all_gather x1, blocking collectives, on_device(): along = lax.all_gather(scattered, 'z')  27.8 us
    pallas_call x1, Pallas kernels, on_device(): pl.pallas_call(factor_kernel, out_shape=(jax.ShapeDtypeStruct((WIDTH, WID...  27.4 us
    all_to_all x1, waiting for transfers between devices, on_device(): gathered = lax.all_to_all(packed, 'pcol', 0, 0, tiled=True)  21.5 us
    all_to_all x1, blocking collectives, on_device(): lax.all_to_all(matrix.reshape(columns, -1, WIDTH), 'pcol', 0, 0, tiled=True)  19.8 us
    all_to_all x1, starting transfers between devices, on_device(): gathered = lax.all_to_all(packed, 'pcol', 0, 0, tiled=True)  12.1 us
    ppermute x1, waiting for transfers between devices, on_device(): other_corner = lax.ppermute(corner, 'yh', swap)  5.95 us
    pallas_call x1, Pallas kernels, on_device(): pl.pallas_call(apply_kernel, out_shape=(jax.ShapeDtypeStruct(matrix.shape...  5.74 us
    ppermute x1, starting transfers between devices, on_device(): other_corner = lax.ppermute(corner, 'yh', swap)  4.53 us
  transfers between devices with their start and end apart: 3, of which 2 were waited for; matrix products, arithmetic and copies ran while one was open for 0% of the time, Pallas kernels for 21%

profile of v1, /device:TPU:1, one launch (start us, length us, event | category | flops | bytes accessed | tf_op | source)
XLA Modules:
  0.0 132.9 jit_solution(11250423129795625362)
XLA Ops:
  0.6 19.8 %all_to_all.10 = f32[16,16,512]{2,1,0:T(8,128)S(1)} all-to-all(f32[16,16,512]{2,1,0:T(8,128)} %bitcast.11), channel_id=1, replica_groups=mesh['z'=16,'yh'=2,'pcol'=16] {'pcol'}, dimensions={0} | all-to-all | bytes 1048576 | tf_op jit(solution)/shard_map/all_to_all | solution.py:148
  20.4 27.8 %all_gather.3 = f32[16,16,512]{2,1,0:T(8,128)S(1)} all-gather(f32[1,16,512]{2,1,0:T(8,128)S(1)} %get-tuple-element.17), channel_id=1, replica_groups=mesh['z'=16,'yh'=2,'pcol'=16] {'z'}, dimensions={0}, use_global_device_ids=true | all-gather | bytes 557056 | tf_op jit(solution)/shard_map/all_gather | solution.py:151
  48.2 0.1 broadcast_in_dim.15
  48.3 0.1 broadcast_in_dim.17
  48.4 1.3 pad_maximum_fusion
  49.7 12.1 %all-to-all-start.1 = ((f32[16,48,512]{2,1,0:T(8,128)}), f32[16,48,512]{2,1,0:T(8,128)S(1)}, u32[]{:S(2)}, u32[]{:S(2)}) async-start(f32[16,48,512]{2,1,0:T(8,128)} %pad_maximum_fusion), calls=%async_computation.1 | async-start | bytes 3145728 | tf_op jit(solution)/shard_map/all_to_all | solution.py:160
  61.8 21.5 %all-to-all-done.1.gathered = f32[16,48,512]{2,1,0:T(8,128)S(1)} async-done(((f32[16,48,512]{2,1,0:T(8,128)}), f32[16,48,512]{2,1,0:T(8,128)S(1)}, u32[]{:S(2)}, u32[]{:S(2)}) %all-to-all-start.1) | async-done | bytes 1572896 | tf_op jit(solution)/shard_map/all_to_all | solution.py:160
  83.2 0.0 copy-start
  83.2 0.1 fusion
  83.4 4.5 %collective-permute-start = (f32[256,256]{1,0:T(8,128)S(1)}, f32[256,256]{1,0:T(8,128)S(1)}, u32[]{:S(2)}, u32[]{:S(2)}) collective-permute-start(f32[256,256]{1,0:T(8,128)S(1)} %constant_dynamic-slice_fusion), channel_id=1, source_target_pairs={{0,16},{16,0},{1,17},{17,1},{2,18},{18,2},{3,19},{19,3},{4,20},{20... | collective-permute-start | bytes 786440 | tf_op jit(solution)/shard_map/ppermute | solution.py:165
  87.9 6.0 %collective-permute-done.other = f32[256,256]{1,0:T(8,128)S(1)} collective-permute-done((f32[256,256]{1,0:T(8,128)S(1)}, f32[256,256]{1,0:T(8,128)S(1)}, u32[]{:S(2)}, u32[]{:S(2)}) %collective-permute-start) | collective-permute-done | bytes 262176 | tf_op jit(solution)/shard_map/ppermute | solution.py:165
  93.9 0.0 copy-start.2
  93.9 4.5 %collective-permute-start.1 = (f32[256,512]{1,0:T(8,128)S(1)}, f32[256,512]{1,0:T(8,128)S(1)}, u32[]{:S(2)}, u32[]{:S(2)}) collective-permute-start(f32[256,512]{1,0:T(8,128)S(1)} %bitcast.13), channel_id=1, source_target_pairs={{0,16},{16,0},{1,17},{17,1},{2,18},{18,2},{3,19},{19,3},{4,20},{20... | collective-permute-start | bytes 1572872 | tf_op jit(solution)/shard_map/ppermute | solution.py:169
  98.4 0.6 pad_add_fusion.place
  99.0 0.0 copy-done
  99.0 0.0 copy-done.2
  99.0 27.4 %factor.1 = (f32[512,512]{1,0:T(8,128)}, f32[1,512]{1,0:T(1,128)}) custom-call(s32[3]{0:T(128)} %pad_add_fusion.place, f32[16,48,512]{2,1,0:T(8,128)} %copy-done, f32[256,256]{1,0:T(8,128)} %copy-done.2), custom_call_target="tpu_custom_call" | custom-call | flops 200000000 | bytes 3000000 | tf_op jit(solution)/shard_map/factor/pallas_call | solution.py:172
  126.4 0.0 collective-permute-done.1.other
  126.4 0.0 copy-start.1
  126.4 0.8 copy-done.1
  127.2 5.7 %apply.1 = (f32[256,512]{1,0:T(8,128)}, f32[16,512]{1,0:T(8,128)}) custom-call(s32[3]{0:T(128)} %pad_add_fusion.place, f32[256,512]{1,0:T(8,128)} %matrix.1, f32[16,48,512]{2,1,0:T(8,128)} %copy-done, f32[256,512]{1,0:T(8,128)} %copy-done.1, f32[512,512]{1,0:T(8,128)} %get-tuple-element.11.inverse, f32[1,512]{1,0:T(1,128)} %get-tuple-element.12.pivots), custom_call_target="tpu_custom_call" | custom-call | flops 400000000 | bytes 5000000 | tf_op jit(solution)/shard_map/apply/pallas_call | solution.py:190
  (3 shorter events, 0.0 us)
Async XLA Ops:
  49.7 33.6 %all-to-all-start.1 = ((f32[16,48,512]{2,1,0:T(8,128)}), f32[16,48,512]{2,1,0:T(8,128)S(1)}, u32[]{:S(2)}, u32[]{:S(2)}) async-start(f32[16,48,512]{2,1,0:T(8,128)} %pad_maximum_fusion), calls=%async_computation.1 | async-start | bytes 3145728 | tf_op jit(solution)/shard_map/all_to_all | solution.py:160
  83.2 15.7 %copy-start = (f32[16,48,512]{2,1,0:T(8,128)}, f32[16,48,512]{2,1,0:T(8,128)S(1)}, u32[]{:S(2)}) copy-start(f32[16,48,512]{2,1,0:T(8,128)S(1)} %all-to-all-done.1.gathered) | copy-start | bytes 4718596
  83.4 10.5 %collective-permute-start = (f32[256,256]{1,0:T(8,128)S(1)}, f32[256,256]{1,0:T(8,128)S(1)}, u32[]{:S(2)}, u32[]{:S(2)}) collective-permute-start(f32[256,256]{1,0:T(8,128)S(1)} %constant_dynamic-slice_fusion), channel_id=1, source_target_pairs={{0,16},{16,0},{1,17},{17,1},{2,18},{18,2},{3,19},{19,3},{4,20},{20... | collective-permute-start | bytes 786440 | tf_op jit(solution)/shard_map/ppermute | solution.py:165
  93.9 5.1 %copy-start.2 = (f32[256,256]{1,0:T(8,128)}, f32[256,256]{1,0:T(8,128)S(1)}, u32[]{:S(2)}) copy-start(f32[256,256]{1,0:T(8,128)S(1)} %collective-permute-done.other) | copy-start | bytes 786436
  93.9 32.5 %collective-permute-start.1 = (f32[256,512]{1,0:T(8,128)S(1)}, f32[256,512]{1,0:T(8,128)S(1)}, u32[]{:S(2)}, u32[]{:S(2)}) collective-permute-start(f32[256,512]{1,0:T(8,128)S(1)} %bitcast.13), channel_id=1, source_target_pairs={{0,16},{16,0},{1,17},{17,1},{2,18},{18,2},{3,19},{19,3},{4,20},{20... | collective-permute-start | bytes 1572872 | tf_op jit(solution)/shard_map/ppermute | solution.py:169
  126.4 0.8 copy-start.1

commit v2 on v1

v2 whole, which is shorter than its diff:
```python
import jax
import jax.numpy as jnp
from jax import lax
from jax.experimental import pallas as pl
from jax.experimental.pallas import tpu as pltpu
from jax.sharding import Mesh
from jax.sharding import PartitionSpec as P

NB = 256
PANELS = 2
WIDTH = NB * PANELS
BLOCK = 128
STEP = 8
PROW = ("z", "yh")
HIGHEST = lax.Precision.HIGHEST


def product(left, right, left_axis, right_axis):
    return lax.dot_general(
        left,
        right,
        (((left_axis,), (right_axis,)), ((), ())),
        precision=HIGHEST,
        preferred_element_type=jnp.float32,
    )


def split(value):
    high = value.astype(jnp.bfloat16).astype(jnp.float32)
    rest = value - high
    middle = rest.astype(jnp.bfloat16).astype(jnp.float32)
    return high, middle, rest - middle


def factor_block(block, reciprocals_out):
    sublane = lax.broadcasted_iota(jnp.int32, (STEP, BLOCK), 0)
    lane = lax.broadcasted_iota(jnp.int32, (STEP, BLOCK), 1)

    def spread_row(value, index):
        return jnp.broadcast_to(value[index : index + 1, :], (STEP, BLOCK))

    def spread_column(value, index):
        return jnp.broadcast_to(value[:, index : index + 1], (STEP, BLOCK))

    pivots = jnp.zeros((STEP, BLOCK), jnp.float32)
    steps = BLOCK // STEP
    columns = None
    for step in range(steps):
        at = STEP * step
        ahead = step < steps - 1
        current = (lane >= at) & (lane < at + STEP)
        rows = block[at : at + STEP, :]
        if columns is None:
            columns = [spread_column(rows, at + j) for j in range(STEP)]
        rows = jnp.where(current, jnp.where(lane == sublane + at, 1.0, 0.0), rows)
        if ahead:
            next_rows = block[at + STEP : at + 2 * STEP, :]
            below = [spread_column(next_rows, at + j) for j in range(STEP)]
            upcoming = [spread_column(next_rows, at + STEP + j) for j in range(STEP)]
            next_rows = jnp.where(current, 0.0, next_rows)
        reciprocals = jnp.zeros((STEP, BLOCK), jnp.float32)
        for k in range(STEP):
            pivot = spread_row(columns[k], k)
            reciprocal = 1.0 / pivot
            factor = jnp.where(sublane > k, columns[k] * reciprocal, 0.0)
            for j in range(k + 1, STEP):
                columns[j] = columns[j] - factor * spread_row(columns[j], k)
            pivot_row = spread_row(rows, k)
            rows = rows - factor * pivot_row
            if ahead:
                below_factor = below[k] * reciprocal
                for j in range(STEP):
                    upcoming[j] = upcoming[j] - below_factor * spread_row(below[k], j)
                for j in range(k + 1, STEP):
                    below[j] = below[j] - below[k] * spread_row(factor, j)
                next_rows = next_rows - below_factor * pivot_row
            reciprocals = jnp.where(sublane == k, reciprocal, reciprocals)
            pivots = jnp.where(lane == at + k, pivot, pivots)
        block[at : at + STEP, :] = rows
        reciprocals_out[at : at + STEP, :] = reciprocals
        if ahead:
            block[at + STEP : at + 2 * STEP, :] = next_rows
            columns = upcoming
        if step < steps - 2:
            later = at + 2 * STEP
            a, b, c = split(rows * reciprocals)
            d, e, f = split(rows)
            change = lax.dot_general(
                jnp.concatenate([a, a, b, b, a, c], axis=0),
                jnp.concatenate([d, e, d, e, f, d], axis=0),
                (((0,), (0,)), ((), ())),
                preferred_element_type=jnp.float32,
            )
            lanes = lax.broadcasted_iota(jnp.int32, (BLOCK - later, BLOCK), 1)
            block[later:, :] = (
                jnp.where((lanes >= at) & (lanes < at + STEP), 0.0, block[later:, :])
                - change[later:, :]
            )
    return pivots[:1, :]


def factor_kernel(gathered, inverse, pivots, work, block, reciprocals):
    half, quarter = NB, BLOCK
    work[:half, :half] = gathered[:16, :, :half].reshape(NB, NB)
    work[half:, half:] = gathered[16:, :, :half].reshape(NB, NB)
    work[half + quarter :, :quarter] = gathered[:8, :, half:].reshape(BLOCK, BLOCK).T
    work[half : half + quarter, quarter:half] = gathered[8:16, :, half:].reshape(BLOCK, BLOCK).T
    work[half : half + quarter, :quarter] = gathered[16:24, :, half:].reshape(BLOCK, BLOCK)
    work[half + quarter :, quarter:half] = gathered[24:, :, half:].reshape(BLOCK, BLOCK)
    inverse[...] = jnp.zeros((WIDTH, WIDTH), jnp.float32)
    lower = lax.broadcasted_iota(jnp.int32, (BLOCK, BLOCK), 0) >= lax.broadcasted_iota(
        jnp.int32, (BLOCK, BLOCK), 1
    )
    for base in range(0, WIDTH, BLOCK):
        end = base + BLOCK
        block[...] = work[base:end, base:end]
        block_pivots = factor_block(block, reciprocals)
        pivots[:, base:end] = block_pivots
        turned = jnp.where(lower, block[...], 0.0)
        scaled = turned * reciprocals[...]
        if end < WIDTH:
            left = product(work[end:, base:end], turned, 1, 1)
            weighed = left / block_pivots
            for at in range(end, WIDTH, BLOCK):
                work[at:, at : at + BLOCK] = work[at:, at : at + BLOCK] - product(
                    left[at - end :], weighed[at - end : at - end + BLOCK], 1, 1
                )
        if base > 0:
            scaled_rows = product(scaled, inverse[base:end, :base], 1, 0)
            inverse[base:end, :base] = product(turned, inverse[base:end, :base], 1, 0)
        inverse[base:end, base:end] = turned
        if end < WIDTH:
            if base > 0:
                inverse[end:, :base] = inverse[end:, :base] - product(left, scaled_rows, 1, 0)
            inverse[end:, base:end] = inverse[end:, base:end] - product(left, scaled, 1, 0)


def apply_kernel(place, matrix, own, across, inverse, pivots, complement, panel, scratch):
    row_block, col_block = place[0], place[1]
    factored = product(own[...].reshape(NB, WIDTH), inverse[...], 1, 1)
    lane = lax.broadcasted_iota(jnp.int32, (NB, WIDTH), 1)
    scratch[...] = jnp.where((row_block == 0) & (lane >= NB), 0.0, factored)
    panel[...] = scratch[pl.ds(pl.multiple_of(16 * col_block, 16), 16), :]
    weighed = product(factored / pivots[...], inverse[...], 1, 0)
    kept = (row_block >= PANELS) & (col_block >= 1)
    change = product(weighed, across[...].reshape(WIDTH, WIDTH), 1, 1)
    complement[...] = jnp.where(kept, matrix[...] - change, 0.0)


def on_device(matrix):
    half = lax.axis_index("yh")
    row_block = lax.axis_index(PROW)
    col_block = lax.axis_index("pcol")
    place = jnp.stack([row_block, col_block]).astype(jnp.int32)
    columns = lax.axis_size("pcol")
    plane = ("yh", "pcol")
    scattered = lax.all_to_all(
        matrix.reshape(columns, -1, WIDTH), "pcol", 0, 0, tiled=True
    )[0]
    copies = jnp.broadcast_to(scattered[None], (columns, *scattered.shape))
    own = lax.all_to_all(copies, "pcol", 0, 0, tiled=True)
    along = lax.all_gather(scattered, "z")
    corner = along[0]
    upper = col_block >= columns // 2
    diagonal = jnp.where(half == 0, corner[:, :NB], corner[:, NB:])
    mine = jnp.where(
        half == 0,
        jnp.where(upper, corner[:, NB : NB + BLOCK], corner[:, NB + BLOCK :]),
        jnp.where(upper, corner[:, BLOCK:NB], corner[:, :BLOCK]),
    )
    piece = jnp.concatenate([diagonal, mine], axis=1)
    gathered = lax.all_to_all(
        jnp.broadcast_to(piece[None], (2 * columns, *piece.shape)), plane, 0, 0, tiled=True
    )
    across = lax.all_to_all(jnp.concatenate([along, along], axis=0), plane, 0, 0, tiled=True)
    smem = pl.BlockSpec(memory_space=pltpu.SMEM)
    vmem = pl.BlockSpec(memory_space=pltpu.VMEM)
    inverse, pivots = pl.pallas_call(
        factor_kernel,
        out_shape=(
            jax.ShapeDtypeStruct((WIDTH, WIDTH), jnp.float32),
            jax.ShapeDtypeStruct((1, WIDTH), jnp.float32),
        ),
        in_specs=[vmem],
        out_specs=(vmem, vmem),
        scratch_shapes=[
            pltpu.VMEM((WIDTH, WIDTH), jnp.float32),
            pltpu.VMEM((BLOCK, BLOCK), jnp.float32),
            pltpu.VMEM((BLOCK, BLOCK), jnp.float32),
        ],
        cost_estimate=pl.CostEstimate(
            flops=200_000_000, bytes_accessed=3_000_000, transcendentals=0
        ),
        name="factor",
    )(gathered)
    complement, panel = pl.pallas_call(
        apply_kernel,
        out_shape=(
            jax.ShapeDtypeStruct(matrix.shape, jnp.float32),
            jax.ShapeDtypeStruct((16, WIDTH), jnp.float32),
        ),
        in_specs=[smem, vmem, vmem, vmem, vmem, vmem],
        out_specs=(vmem, vmem),
        scratch_shapes=[pltpu.VMEM((NB, WIDTH), jnp.float32)],
        cost_estimate=pl.CostEstimate(
            flops=400_000_000, bytes_accessed=5_000_000, transcendentals=0
        ),
        name="apply",
    )(place, matrix, own, across, inverse, pivots)
    return complement, panel, pivots.reshape(WIDTH)


def solution(mesh):
    split = Mesh(mesh.devices.reshape(16, 2, mesh.shape["pcol"]), ("z", "yh", "pcol"))
    return jax.shard_map(
        on_device,
        mesh=split,
        in_specs=(P(PROW, "pcol"),),
        out_specs=(P(PROW, "pcol"), P((*PROW, "pcol"), None), P()),
        check_vma=False,
    )
```

time: 133 us -> 122 us (0.917)
  blocking collectives: 47.6 us -> 27.8 us
  starting transfers between devices: 21.1 us -> 32 us
  Pallas kernels: 33.1 us -> 23.4 us
  waiting for transfers between devices: 27.4 us -> 32.3 us
  local copies, waits for them, and re-layouts: 1.03 us -> 3.82 us
    all_to_all x1 -> x4, starting transfers between devices: 12.1 us -> 32 us  [the longest x1 12 us: on_device(): own = lax.all_to_all(copies, 'pcol', 0, 0, tiled=True)]
    all_to_all x1 -> x0, blocking collectives: 19.8 us -> none  [on_device(): lax.all_to_all(matrix.reshape(columns, -1, WIDTH), 'pcol', 0, 0, tiled=True)]
    all_to_all x1 -> x4, waiting for transfers between devices: 21.5 us -> 32.3 us  [the longest x1 13.1 us: on_device(): lax.all_to_all(jnp.broadcast_to(piece[None], (2 * columns, *piece.shape))...]
    pallas_call x1, Pallas kernels: 27.4 us -> 17.8 us  [on_device(): pl.pallas_call(factor_kernel, out_shape=(jax.ShapeDtypeStruct((WIDTH, WID...]
    ppermute x2 -> x0, starting transfers between devices: 9.05 us -> none  [the longest x1 4.53 us: on_device(): other_corner = lax.ppermute(corner, 'yh', swap)]
    ppermute x2 -> x0, waiting for transfers between devices: 5.96 us -> none  [the longest x1 5.95 us: on_device(): other_corner = lax.ppermute(corner, 'yh', swap)]
    broadcast_in_dim x3 -> x2, local copies, waits for them, and re-layouts: 0.11 us -> 1.9 us  [the longest x1 1.05 us: on_device(): jnp.broadcast_to(piece[None], (2 * columns, *piece.shape))]
  transfers between devices with their start and end apart: 3 -> 4, of which waited for: 2 -> 3; matrix products, arithmetic and copies ran while one was open for 0% -> 1% of each run, Pallas kernels for 21% -> 15%
where the time goes in v2:
time: 122 us
  waiting for transfers between devices  32.3 us (26%)
  starting transfers between devices  32 us (26%)
  blocking collectives  27.8 us (23%)
  Pallas kernels  23.4 us (19%)
  local copies, waits for them, and re-layouts  3.82 us (3%)
  other arithmetic  1.71 us (1%)
    all_gather x1, blocking collectives, on_device(): along = lax.all_gather(scattered, 'z')  27.8 us
    pallas_call x1, Pallas kernels, on_device(): pl.pallas_call(factor_kernel, out_shape=(jax.ShapeDtypeStruct((WIDTH, WID...  17.8 us
    all_to_all x1, waiting for transfers between devices, on_device(): lax.all_to_all(jnp.broadcast_to(piece[None], (2 * columns, *piece.shape))...  13.1 us
    all_to_all x1, starting transfers between devices, on_device(): own = lax.all_to_all(copies, 'pcol', 0, 0, tiled=True)  12 us
    all_to_all x1, starting transfers between devices, on_device(): lax.all_to_all(matrix.reshape(columns, -1, WIDTH), 'pcol', 0, 0, tiled=True)  10.2 us
    all_to_all x1, waiting for transfers between devices, on_device(): lax.all_to_all(matrix.reshape(columns, -1, WIDTH), 'pcol', 0, 0, tiled=True)  9.6 us
    all_to_all x1, waiting for transfers between devices, on_device(): own = lax.all_to_all(copies, 'pcol', 0, 0, tiled=True)  9.56 us
    all_to_all x1, starting transfers between devices, on_device(): lax.all_to_all(jnp.broadcast_to(piece[None], (2 * columns, *piece.shape))...  5.75 us
  transfers between devices with their start and end apart: 4, of which 3 were waited for; matrix products, arithmetic and copies ran while one was open for 1% of the time, Pallas kernels for 15%

profile of v2, /device:TPU:1, one launch (start us, length us, event | category | flops | bytes accessed | tf_op | source)
XLA Modules:
  0.0 121.7 jit_solution(14776233667460281482)
XLA Ops:
  0.6 10.2 %all-to-all-start = ((f32[16,16,512]{2,1,0:T(8,128)}), f32[16,16,512]{2,1,0:T(8,128)S(1)}, u32[]{:S(2)}, u32[]{:S(2)}) async-start(f32[16,16,512]{2,1,0:T(8,128)} %bitcast.8), calls=%async_computation | async-start | bytes 1048576 | tf_op jit(solution)/shard_map/all_to_all | solution.py:157
  10.8 9.6 %all-to-all-done = f32[16,16,512]{2,1,0:T(8,128)S(1)} async-done(((f32[16,16,512]{2,1,0:T(8,128)}), f32[16,16,512]{2,1,0:T(8,128)S(1)}, u32[]{:S(2)}, u32[]{:S(2)}) %all-to-all-start) | async-done | bytes 524320 | tf_op jit(solution)/shard_map/all_to_all | solution.py:157
  20.4 27.8 %all_gather.3 = f32[16,16,512]{2,1,0:T(8,128)S(1)} all-gather(f32[1,16,512]{2,1,0:T(8,128)S(1)} %get-tuple-element.11), channel_id=1, replica_groups=mesh['z'=16,'yh'=2,'pcol'=16] {'z'}, dimensions={0}, use_global_device_ids=true | all-gather | bytes 557056 | tf_op jit(solution)/shard_map/all_gather | solution.py:162
  48.2 0.9 broadcast_in_dim.14
  49.1 12.0 %all-to-all-start.1 = ((f32[16,16,512]{2,1,0:T(8,128)}), f32[16,16,512]{2,1,0:T(8,128)S(1)}, u32[]{:S(2)}, u32[]{:S(2)}) async-start(f32[16,16,512]{2,1,0:T(8,128)} %broadcast_in_dim.14), calls=%async_computation.1 | async-start | bytes 1048576 | tf_op jit(solution)/shard_map/all_to_all | solution.py:161
  61.1 9.6 %all-to-all-done.1.own = f32[16,16,512]{2,1,0:T(8,128)S(1)} async-done(((f32[16,16,512]{2,1,0:T(8,128)}), f32[16,16,512]{2,1,0:T(8,128)S(1)}, u32[]{:S(2)}, u32[]{:S(2)}) %all-to-all-start.1) | async-done | bytes 524320 | tf_op jit(solution)/shard_map/all_to_all | solution.py:161
  70.6 0.0 copy-start.2
  70.6 1.0 broadcast_in_dim.15
  71.7 0.0 copy-done.2
  71.7 5.8 %all-to-all-start.3 = ((f32[32,16,384]{2,1,0:T(8,128)}), f32[32,16,384]{2,1,0:T(8,128)S(1)}, u32[]{:S(2)}, u32[]{:S(2)}) async-start(f32[32,16,384]{2,1,0:T(8,128)} %broadcast_in_dim.15), calls=%async_computation.3 | async-start | bytes 1572864 | tf_op jit(solution)/shard_map/all_to_all | solution.py:172
  77.5 1.1 pad_maximum_fusion
  78.6 13.1 %all-to-all-done.3.gathered = f32[32,16,384]{2,1,0:T(8,128)S(1)} async-done(((f32[32,16,384]{2,1,0:T(8,128)}), f32[32,16,384]{2,1,0:T(8,128)S(1)}, u32[]{:S(2)}, u32[]{:S(2)}) %all-to-all-start.3) | async-done | bytes 786464 | tf_op jit(solution)/shard_map/all_to_all | solution.py:172
  91.7 0.0 copy-start.1
  91.7 0.9 copy-done.1
  92.6 4.1 %all-to-all-start.2 = ((f32[32,16,512]{2,1,0:T(8,128)}), f32[32,16,512]{2,1,0:T(8,128)S(1)}, u32[]{:S(2)}, u32[]{:S(2)}) async-start(f32[32,16,512]{2,1,0:T(8,128)} %pad_maximum_fusion), calls=%async_computation.2 | async-start | bytes 2097152 | tf_op jit(solution)/shard_map/all_to_all | solution.py:175
  96.8 0.6 pad_add_fusion.place
  97.3 17.8 %factor.1 = (f32[512,512]{1,0:T(8,128)}, f32[1,512]{1,0:T(1,128)}) custom-call(f32[32,16,384]{2,1,0:T(8,128)} %copy-done.1), custom_call_target="tpu_custom_call" | custom-call | flops 200000000 | bytes 3000000 | tf_op jit(solution)/shard_map/factor/pallas_call | solution.py:178
  115.2 0.0 all-to-all-done.2.across
  115.2 0.0 copy-start
  115.2 1.0 copy-done
  116.2 5.6 %apply.1 = (f32[256,512]{1,0:T(8,128)}, f32[16,512]{1,0:T(8,128)}) custom-call(s32[2]{0:T(128)} %pad_add_fusion.place, f32[256,512]{1,0:T(8,128)} %matrix.1, f32[16,16,512]{2,1,0:T(8,128)} %copy-done.2, f32[32,16,512]{2,1,0:T(8,128)} %copy-done, f32[512,512]{1,0:T(8,128)} %get-tuple-element.7.inverse, f32[1,512]{1,0:T(1,128)} %get-tuple-element.8.pivots), custom_call_target="tpu_custom_call" | custom-call | flops 400000000 | bytes 5000000 | tf_op jit(solution)/shard_map/apply/pallas_call | solution.py:196
  (5 shorter events, 0.0 us)
Async XLA Ops:
  0.6 19.8 %all-to-all-start = ((f32[16,16,512]{2,1,0:T(8,128)}), f32[16,16,512]{2,1,0:T(8,128)S(1)}, u32[]{:S(2)}, u32[]{:S(2)}) async-start(f32[16,16,512]{2,1,0:T(8,128)} %bitcast.8), calls=%async_computation | async-start | bytes 1048576 | tf_op jit(solution)/shard_map/all_to_all | solution.py:157
  49.1 21.6 %all-to-all-start.1 = ((f32[16,16,512]{2,1,0:T(8,128)}), f32[16,16,512]{2,1,0:T(8,128)S(1)}, u32[]{:S(2)}, u32[]{:S(2)}) async-start(f32[16,16,512]{2,1,0:T(8,128)} %broadcast_in_dim.14), calls=%async_computation.1 | async-start | bytes 1048576 | tf_op jit(solution)/shard_map/all_to_all | solution.py:161
  70.6 1.1 copy-start.2
  71.7 20.0 %all-to-all-start.3 = ((f32[32,16,384]{2,1,0:T(8,128)}), f32[32,16,384]{2,1,0:T(8,128)S(1)}, u32[]{:S(2)}, u32[]{:S(2)}) async-start(f32[32,16,384]{2,1,0:T(8,128)} %broadcast_in_dim.15), calls=%async_computation.3 | async-start | bytes 1572864 | tf_op jit(solution)/shard_map/all_to_all | solution.py:172
  91.7 0.9 copy-start.1
  92.6 22.5 %all-to-all-start.2 = ((f32[32,16,512]{2,1,0:T(8,128)}), f32[32,16,512]{2,1,0:T(8,128)S(1)}, u32[]{:S(2)}, u32[]{:S(2)}) async-start(f32[32,16,512]{2,1,0:T(8,128)} %pad_maximum_fusion), calls=%async_computation.2 | async-start | bytes 2097152 | tf_op jit(solution)/shard_map/all_to_all | solution.py:175
  115.2 1.0 copy-start

commit v3 on v2

--- a/solution.py
+++ b/solution.py
@@ -135,16 +135,36 @@
             inverse[end:, base:end] = inverse[end:, base:end] - product(left, scaled, 1, 0)
 
 
-def apply_kernel(place, matrix, own, across, inverse, pivots, complement, panel, scratch):
+def apply_kernel(
+    place, matrix, own, across, inverse, pivots, complement, panel, factored, weighed, local, arrived
+):
+    fetch = pltpu.make_async_copy(matrix, local, arrived)
+    fetch.start()
     row_block, col_block = place[0], place[1]
-    factored = product(own[...].reshape(NB, WIDTH), inverse[...], 1, 1)
-    lane = lax.broadcasted_iota(jnp.int32, (NB, WIDTH), 1)
-    scratch[...] = jnp.where((row_block == 0) & (lane >= NB), 0.0, factored)
-    panel[...] = scratch[pl.ds(pl.multiple_of(16 * col_block, 16), 16), :]
-    weighed = product(factored / pivots[...], inverse[...], 1, 0)
+    rows = own[...].reshape(NB, WIDTH)
+    for base in range(0, WIDTH, BLOCK):
+        end = base + BLOCK
+        part = product(rows[:, :end], inverse[base:end, :end], 1, 1)
+        weighed[:, base:end] = part / pivots[:, base:end]
+        if base >= NB:
+            part = jnp.where(row_block == 0, 0.0, part)
+        factored[:, base:end] = part
+    panel[...] = factored[pl.ds(pl.multiple_of(16 * col_block, 16), 16), :]
+    turned = jnp.concatenate(
+        [
+            product(weighed[:, base:], inverse[base:, base : base + BLOCK], 1, 0)
+            for base in range(0, WIDTH, BLOCK)
+        ],
+        axis=1,
+    )
+    change = product(turned, across[...].reshape(WIDTH, WIDTH), 1, 1)
+    fetch.wait()
     kept = (row_block >= PANELS) & (col_block >= 1)
-    change = product(weighed, across[...].reshape(WIDTH, WIDTH), 1, 1)
-    complement[...] = jnp.where(kept, matrix[...] - change, 0.0)
+    complement[...] = jnp.where(kept, local[...] - change, 0.0)
+
+
+def in_vmem(array):
+    return pltpu.with_memory_space_constraint(array, pltpu.VMEM)
 
 
 def on_device(matrix):
@@ -178,7 +198,7 @@
     inverse, pivots = pl.pallas_call(
         factor_kernel,
         out_shape=(
-            jax.ShapeDtypeStruct((WIDTH, WIDTH), jnp.float32),
+            pltpu.VMEM((WIDTH, WIDTH), jnp.float32),
             jax.ShapeDtypeStruct((1, WIDTH), jnp.float32),
         ),
         in_specs=[vmem],
@@ -192,21 +212,26 @@
             flops=200_000_000, bytes_accessed=3_000_000, transcendentals=0
         ),
         name="factor",
-    )(gathered)
+    )(in_vmem(gathered))
     complement, panel = pl.pallas_call(
         apply_kernel,
         out_shape=(
             jax.ShapeDtypeStruct(matrix.shape, jnp.float32),
             jax.ShapeDtypeStruct((16, WIDTH), jnp.float32),
         ),
-        in_specs=[smem, vmem, vmem, vmem, vmem, vmem],
+        in_specs=[smem, pl.BlockSpec(memory_space=pl.ANY), vmem, vmem, vmem, vmem],
         out_specs=(vmem, vmem),
-        scratch_shapes=[pltpu.VMEM((NB, WIDTH), jnp.float32)],
+        scratch_shapes=[
+            pltpu.VMEM((NB, WIDTH), jnp.float32),
+            pltpu.VMEM((NB, WIDTH), jnp.float32),
+            pltpu.VMEM((NB, WIDTH), jnp.float32),
+            pltpu.SemaphoreType.DMA(()),
+        ],
         cost_estimate=pl.CostEstimate(
             flops=400_000_000, bytes_accessed=5_000_000, transcendentals=0
         ),
         name="apply",
-    )(place, matrix, own, across, inverse, pivots)
+    )(place, matrix, in_vmem(own), in_vmem(across), in_vmem(inverse), pivots)
     return complement, panel, pivots.reshape(WIDTH)
 
 

time: 122 us -> 119 us (0.975)
  local copies, waits for them, and re-layouts: 3.82 us -> 1.86 us
  Pallas kernels: 23.4 us -> 21.5 us
    unnamed x6 -> x0, local copies, waits for them, and re-layouts: 1.91 us -> none
    pallas_call x1, Pallas kernels: 17.8 us -> 16 us  [on_device(): pl.pallas_call(factor_kernel, out_shape=(pltpu.VMEM((WIDTH, WIDTH), jnp.f...]
  transfers between devices with their start and end apart: 4 -> 4, of which waited for: 3 -> 4; matrix products, arithmetic and copies ran while one was open for 1% -> 1% of each run, Pallas kernels for 15% -> 13%
where the time goes in v3:
time: 119 us; the launch traced here: 118 us
  waiting for transfers between devices  32.9 us (28%)
  starting transfers between devices  32 us (27%)
  blocking collectives  27.8 us (23%)
  Pallas kernels  21.5 us (18%)
  local copies, waits for them, and re-layouts  1.86 us (2%)
  other arithmetic  1.73 us (1%)
    all_gather x1, blocking collectives, on_device(): along = lax.all_gather(scattered, 'z')  27.8 us
    pallas_call x1, Pallas kernels, on_device(): pl.pallas_call(factor_kernel, out_shape=(pltpu.VMEM((WIDTH, WIDTH), jnp.f...  16 us
    all_to_all x1, waiting for transfers between devices, on_device(): lax.all_to_all(jnp.broadcast_to(piece[None], (2 * columns, *piece.shape))...  13.1 us
    all_to_all x1, starting transfers between devices, on_device(): own = lax.all_to_all(copies, 'pcol', 0, 0, tiled=True)  12 us
    all_to_all x1, starting transfers between devices, on_device(): lax.all_to_all(matrix.reshape(columns, -1, WIDTH), 'pcol', 0, 0, tiled=True)  10.2 us
    all_to_all x1, waiting for transfers between devices, on_device(): lax.all_to_all(matrix.reshape(columns, -1, WIDTH), 'pcol', 0, 0, tiled=True)  9.6 us
    all_to_all x1, waiting for transfers between devices, on_device(): own = lax.all_to_all(copies, 'pcol', 0, 0, tiled=True)  9.56 us
    all_to_all x1, starting transfers between devices, on_device(): lax.all_to_all(jnp.broadcast_to(piece[None], (2 * columns, *piece.shape))...  5.75 us
  transfers between devices with their start and end apart: 4, of which 4 were waited for; matrix products, arithmetic and copies ran while one was open for 1% of the time, Pallas kernels for 13%

profile of v3, /device:TPU:1, one launch (start us, length us, event | category | flops | bytes accessed | tf_op | source)
XLA Modules:
  0.0 118.4 jit_solution(1954886328541437489)
XLA Ops:
  0.6 10.2 %all-to-all-start = ((f32[16,16,512]{2,1,0:T(8,128)}), f32[16,16,512]{2,1,0:T(8,128)S(1)}, u32[]{:S(2)}, u32[]{:S(2)}) async-start(f32[16,16,512]{2,1,0:T(8,128)} %bitcast.8), calls=%async_computation | async-start | bytes 1048576 | tf_op jit(solution)/shard_map/all_to_all | solution.py:177
  10.8 9.6 %all-to-all-done = f32[16,16,512]{2,1,0:T(8,128)S(1)} async-done(((f32[16,16,512]{2,1,0:T(8,128)}), f32[16,16,512]{2,1,0:T(8,128)S(1)}, u32[]{:S(2)}, u32[]{:S(2)}) %all-to-all-start) | async-done | bytes 524320 | tf_op jit(solution)/shard_map/all_to_all | solution.py:177
  20.4 27.8 %all_gather.3 = f32[16,16,512]{2,1,0:T(8,128)S(1)} all-gather(f32[1,16,512]{2,1,0:T(8,128)S(1)} %get-tuple-element.11), channel_id=1, replica_groups=mesh['z'=16,'yh'=2,'pcol'=16] {'z'}, dimensions={0}, use_global_device_ids=true | all-gather | bytes 557056 | tf_op jit(solution)/shard_map/all_gather | solution.py:182
  48.2 0.9 broadcast_in_dim.14
  49.1 12.0 %all-to-all-start.1 = ((f32[16,16,512]{2,1,0:T(8,128)}), f32[16,16,512]{2,1,0:T(8,128)S(1)}, u32[]{:S(2)}, u32[]{:S(2)}) async-start(f32[16,16,512]{2,1,0:T(8,128)} %broadcast_in_dim.14), calls=%async_computation.1 | async-start | bytes 1048576 | tf_op jit(solution)/shard_map/all_to_all | solution.py:181
  61.1 9.6 %all-to-all-done.1.own = f32[16,16,512]{2,1,0:T(8,128)S(1)} async-done(((f32[16,16,512]{2,1,0:T(8,128)}), f32[16,16,512]{2,1,0:T(8,128)S(1)}, u32[]{:S(2)}, u32[]{:S(2)}) %all-to-all-start.1) | async-done | bytes 524320 | tf_op jit(solution)/shard_map/all_to_all | solution.py:181
  70.6 1.0 broadcast_in_dim.15
  71.6 5.8 %all-to-all-start.3 = ((f32[32,16,384]{2,1,0:T(8,128)}), f32[32,16,384]{2,1,0:T(8,128)S(1)}, u32[]{:S(2)}, u32[]{:S(2)}) async-start(f32[32,16,384]{2,1,0:T(8,128)} %broadcast_in_dim.15), calls=%async_computation.3 | async-start | bytes 1572864 | tf_op jit(solution)/shard_map/all_to_all | solution.py:192
  77.4 1.1 pad_maximum_fusion
  78.5 13.1 %all-to-all-done.3.gathered = f32[32,16,384]{2,1,0:T(8,128)S(1)} async-done(((f32[32,16,384]{2,1,0:T(8,128)}), f32[32,16,384]{2,1,0:T(8,128)S(1)}, u32[]{:S(2)}, u32[]{:S(2)}) %all-to-all-start.3) | async-done | bytes 786464 | tf_op jit(solution)/shard_map/all_to_all | solution.py:192
  91.6 4.1 %all-to-all-start.2 = ((f32[32,16,512]{2,1,0:T(8,128)}), f32[32,16,512]{2,1,0:T(8,128)S(1)}, u32[]{:S(2)}, u32[]{:S(2)}) async-start(f32[32,16,512]{2,1,0:T(8,128)} %pad_maximum_fusion), calls=%async_computation.2 | async-start | bytes 2097152 | tf_op jit(solution)/shard_map/all_to_all | solution.py:195
  95.8 0.6 pad_add_fusion.place
  96.4 16.0 %factor.1 = (f32[512,512]{1,0:T(8,128)S(1)}, f32[1,512]{1,0:T(1,128)}) custom-call(f32[32,16,384]{2,1,0:T(8,128)S(1)} %all-to-all-done.3.gathered), custom_call_target="tpu_custom_call" | custom-call | flops 200000000 | bytes 3000000 | tf_op jit(solution)/shard_map/factor/pallas_call | solution.py:198
  112.3 0.6 all-to-all-done.2.across
  112.9 5.5 %apply.1 = (f32[256,512]{1,0:T(8,128)}, f32[16,512]{1,0:T(8,128)}) custom-call(s32[2]{0:T(128)} %pad_add_fusion.place, f32[256,512]{1,0:T(8,128)} %matrix.1, f32[16,16,512]{2,1,0:T(8,128)S(1)} %all-to-all-done.1.own, f32[32,16,512]{2,1,0:T(8,128)S(1)} %all-to-all-done.2.across, f32[512,512]{1,0:T(8,128)S(1)} %get-tuple-element.7.inverse, ...), custom_call_target="tpu_custom_call" | custom-call | flops 400000000 | bytes 5000000 | tf_op jit(solution)/shard_map/apply/pallas_call | solution.py:216
  (5 shorter events, 0.0 us)
Async XLA Ops:
  0.6 19.8 %all-to-all-start = ((f32[16,16,512]{2,1,0:T(8,128)}), f32[16,16,512]{2,1,0:T(8,128)S(1)}, u32[]{:S(2)}, u32[]{:S(2)}) async-start(f32[16,16,512]{2,1,0:T(8,128)} %bitcast.8), calls=%async_computation | async-start | bytes 1048576 | tf_op jit(solution)/shard_map/all_to_all | solution.py:177
  49.1 21.6 %all-to-all-start.1 = ((f32[16,16,512]{2,1,0:T(8,128)}), f32[16,16,512]{2,1,0:T(8,128)S(1)}, u32[]{:S(2)}, u32[]{:S(2)}) async-start(f32[16,16,512]{2,1,0:T(8,128)} %broadcast_in_dim.14), calls=%async_computation.1 | async-start | bytes 1048576 | tf_op jit(solution)/shard_map/all_to_all | solution.py:181
  71.6 20.0 %all-to-all-start.3 = ((f32[32,16,384]{2,1,0:T(8,128)}), f32[32,16,384]{2,1,0:T(8,128)S(1)}, u32[]{:S(2)}, u32[]{:S(2)}) async-start(f32[32,16,384]{2,1,0:T(8,128)} %broadcast_in_dim.15), calls=%async_computation.3 | async-start | bytes 1572864 | tf_op jit(solution)/shard_map/all_to_all | solution.py:192
  91.6 21.3 %all-to-all-start.2 = ((f32[32,16,512]{2,1,0:T(8,128)}), f32[32,16,512]{2,1,0:T(8,128)S(1)}, u32[]{:S(2)}, u32[]{:S(2)}) async-start(f32[32,16,512]{2,1,0:T(8,128)} %pad_maximum_fusion), calls=%async_computation.2 | async-start | bytes 2097152 | tf_op jit(solution)/shard_map/all_to_all | solution.py:195

commit v4 on v3

--- a/solution.py
+++ b/solution.py
@@ -99,18 +99,28 @@
     return pivots[:1, :]
 
 
-def factor_kernel(gathered, inverse, pivots, work, block, reciprocals):
+def factor_kernel(
+    place, gathered, own, turned_rows, pivots, panel, corner, work, inverse, factored, block, reciprocals
+):
+    row_block, col_block, odd = place[0], place[1], place[2]
+    for at in range(0, 2 * 16, 2):
+        for side in range(2):
+            corner[16 * (at + side) : 16 * (at + side + 1), :] = gathered[
+                at + jnp.where(odd == 1, 1 - side, side)
+            ]
     half, quarter = NB, BLOCK
-    work[:half, :half] = gathered[:16, :, :half].reshape(NB, NB)
-    work[half:, half:] = gathered[16:, :, :half].reshape(NB, NB)
-    work[half + quarter :, :quarter] = gathered[:8, :, half:].reshape(BLOCK, BLOCK).T
-    work[half : half + quarter, quarter:half] = gathered[8:16, :, half:].reshape(BLOCK, BLOCK).T
-    work[half : half + quarter, :quarter] = gathered[16:24, :, half:].reshape(BLOCK, BLOCK)
-    work[half + quarter :, quarter:half] = gathered[24:, :, half:].reshape(BLOCK, BLOCK)
+    work[:half, :half] = corner[:half, :half]
+    work[half:, half:] = corner[half:, :half]
+    work[half + quarter :, :quarter] = corner[:quarter, half:].T
+    work[half : half + quarter, quarter:half] = corner[quarter:half, half:].T
+    work[half : half + quarter, :quarter] = corner[half : half + quarter, half:]
+    work[half + quarter :, quarter:half] = corner[half + quarter :, half:]
     inverse[...] = jnp.zeros((WIDTH, WIDTH), jnp.float32)
+    turned_rows[...] = jnp.zeros((NB, WIDTH), jnp.float32)
     lower = lax.broadcasted_iota(jnp.int32, (BLOCK, BLOCK), 0) >= lax.broadcasted_iota(
         jnp.int32, (BLOCK, BLOCK), 1
     )
+    rows = own[...].reshape(NB, WIDTH)
     for base in range(0, WIDTH, BLOCK):
         end = base + BLOCK
         block[...] = work[base:end, base:end]
@@ -133,31 +143,26 @@
             if base > 0:
                 inverse[end:, :base] = inverse[end:, :base] - product(left, scaled_rows, 1, 0)
             inverse[end:, base:end] = inverse[end:, base:end] - product(left, scaled, 1, 0)
-
-
-def apply_kernel(
-    place, matrix, own, across, inverse, pivots, complement, panel, factored, weighed, local, arrived
-):
-    fetch = pltpu.make_async_copy(matrix, local, arrived)
-    fetch.start()
-    row_block, col_block = place[0], place[1]
-    rows = own[...].reshape(NB, WIDTH)
-    for base in range(0, WIDTH, BLOCK):
-        end = base + BLOCK
         part = product(rows[:, :end], inverse[base:end, :end], 1, 1)
-        weighed[:, base:end] = part / pivots[:, base:end]
+        turned_rows[:, :end] = turned_rows[:, :end] + product(
+            part / block_pivots, inverse[base:end, :end], 1, 0
+        )
         if base >= NB:
             part = jnp.where(row_block == 0, 0.0, part)
         factored[:, base:end] = part
     panel[...] = factored[pl.ds(pl.multiple_of(16 * col_block, 16), 16), :]
-    turned = jnp.concatenate(
-        [
-            product(weighed[:, base:], inverse[base:, base : base + BLOCK], 1, 0)
-            for base in range(0, WIDTH, BLOCK)
-        ],
-        axis=1,
-    )
-    change = product(turned, across[...].reshape(WIDTH, WIDTH), 1, 1)
+
+
+def apply_kernel(place, matrix, across, turned_rows, complement, ordered, local, arrived):
+    fetch = pltpu.make_async_copy(matrix, local, arrived)
+    fetch.start()
+    row_block, col_block, swapped = place[0], place[1], place[3]
+    for at in range(0, 2 * 16, 2):
+        for side in range(2):
+            ordered[16 * (at + side) : 16 * (at + side + 1), :] = across[
+                at + jnp.where(swapped == 1, 1 - side, side)
+            ]
+    change = product(turned_rows[...], ordered[...], 1, 1)
     fetch.wait()
     kept = (row_block >= PANELS) & (col_block >= 1)
     complement[...] = jnp.where(kept, local[...] - change, 0.0)
@@ -171,7 +176,9 @@
     half = lax.axis_index("yh")
     row_block = lax.axis_index(PROW)
     col_block = lax.axis_index("pcol")
-    place = jnp.stack([row_block, col_block]).astype(jnp.int32)
+    depth = lax.axis_index("z")
+    place = jnp.stack([row_block, col_block, depth % 2, (depth + col_block) % 2])
+    place = place.astype(jnp.int32)
     columns = lax.axis_size("pcol")
     plane = ("yh", "pcol")
     scattered = lax.all_to_all(
@@ -179,7 +186,15 @@
     )[0]
     copies = jnp.broadcast_to(scattered[None], (columns, *scattered.shape))
     own = lax.all_to_all(copies, "pcol", 0, 0, tiled=True)
-    along = lax.all_gather(scattered, "z")
+    along = lax.all_gather(
+        scattered,
+        ("z", "pcol"),
+        axis_index_groups=[
+            [z * columns + at + (z + side) % 2 for z in range(lax.axis_size("z"))]
+            for at in range(0, columns, 2)
+            for side in range(2)
+        ],
+    )
     corner = along[0]
     upper = col_block >= columns // 2
     diagonal = jnp.where(half == 0, corner[:, :NB], corner[:, NB:])
@@ -195,43 +210,43 @@
     across = lax.all_to_all(jnp.concatenate([along, along], axis=0), plane, 0, 0, tiled=True)
     smem = pl.BlockSpec(memory_space=pltpu.SMEM)
     vmem = pl.BlockSpec(memory_space=pltpu.VMEM)
-    inverse, pivots = pl.pallas_call(
+    turned_rows, pivots, panel = pl.pallas_call(
         factor_kernel,
         out_shape=(
+            pltpu.VMEM((NB, WIDTH), jnp.float32),
+            jax.ShapeDtypeStruct((1, WIDTH), jnp.float32),
+            jax.ShapeDtypeStruct((16, WIDTH), jnp.float32),
+        ),
+        in_specs=[smem, vmem, vmem],
+        out_specs=(vmem, vmem, vmem),
+        scratch_shapes=[
+            pltpu.VMEM((WIDTH, NB + BLOCK), jnp.float32),
             pltpu.VMEM((WIDTH, WIDTH), jnp.float32),
-            jax.ShapeDtypeStruct((1, WIDTH), jnp.float32),
-        ),
-        in_specs=[vmem],
-        out_specs=(vmem, vmem),
-        scratch_shapes=[
             pltpu.VMEM((WIDTH, WIDTH), jnp.float32),
+            pltpu.VMEM((NB, WIDTH), jnp.float32),
             pltpu.VMEM((BLOCK, BLOCK), jnp.float32),
             pltpu.VMEM((BLOCK, BLOCK), jnp.float32),
         ],
         cost_estimate=pl.CostEstimate(
-            flops=200_000_000, bytes_accessed=3_000_000, transcendentals=0
+            flops=400_000_000, bytes_accessed=3_000_000, transcendentals=0
         ),
         name="factor",
-    )(in_vmem(gathered))
-    complement, panel = pl.pallas_call(
+    )(place, in_vmem(gathered), in_vmem(own))
+    complement = pl.pallas_call(
         apply_kernel,
-        out_shape=(
-            jax.ShapeDtypeStruct(matrix.shape, jnp.float32),
-            jax.ShapeDtypeStruct((16, WIDTH), jnp.float32),
-        ),
-        in_specs=[smem, pl.BlockSpec(memory_space=pl.ANY), vmem, vmem, vmem, vmem],
-        out_specs=(vmem, vmem),
+        out_shape=jax.ShapeDtypeStruct(matrix.shape, jnp.float32),
+        in_specs=[smem, pl.BlockSpec(memory_space=pl.ANY), vmem, vmem],
+        out_specs=vmem,
         scratch_shapes=[
-            pltpu.VMEM((NB, WIDTH), jnp.float32),
-            pltpu.VMEM((NB, WIDTH), jnp.float32),
+            pltpu.VMEM((WIDTH, WIDTH), jnp.float32),
             pltpu.VMEM((NB, WIDTH), jnp.float32),
             pltpu.SemaphoreType.DMA(()),
         ],
         cost_estimate=pl.CostEstimate(
-            flops=400_000_000, bytes_accessed=5_000_000, transcendentals=0
+            flops=200_000_000, bytes_accessed=3_000_000, transcendentals=0
         ),
         name="apply",
-    )(place, matrix, in_vmem(own), in_vmem(across), in_vmem(inverse), pivots)
+    )(place, matrix, in_vmem(across), in_vmem(turned_rows))
     return complement, panel, pivots.reshape(WIDTH)
 
 

time: 119 us -> 115 us (0.966)
  starting transfers between devices: 32 us -> 23.6 us
  blocking collectives: 27.8 us -> 32.3 us
  waiting for transfers between devices: 32.9 us -> 31.5 us
  Pallas kernels: 21.5 us -> 22.8 us
    all_to_all x1, starting transfers between devices: 12 us -> 3.47 us  [on_device(): own = lax.all_to_all(copies, 'pcol', 0, 0, tiled=True)]
    all_gather x1, blocking collectives: 27.8 us -> 32.3 us  [on_device(): lax.all_gather(scattered, ('z', 'pcol'), axis_index_groups=[[z * columns...]
    pallas_call x2, Pallas kernels: 21.5 us -> 22.8 us  [the longest x1 19.7 us: on_device(): pl.pallas_call(factor_kernel, out_shape=(pltpu.VMEM((NB, WIDTH), jnp.floa...]
  transfers between devices with their start and end apart: 4 -> 4, of which waited for: 4 -> 3; matrix products, arithmetic and copies ran while one was open for 1% -> 2% of each run, Pallas kernels for 13% -> 17%
where the time goes in v4:
time: 115 us; the launch traced here: 114 us
  blocking collectives  32.3 us (28%)
  waiting for transfers between devices  31.5 us (27%)
  starting transfers between devices  23.6 us (21%)
  Pallas kernels  22.8 us (20%)
  local copies, waits for them, and re-layouts  1.84 us (2%)
  other arithmetic  1.73 us (2%)
    all_gather x1, blocking collectives, on_device(): lax.all_gather(scattered, ('z', 'pcol'), axis_index_groups=[[z * columns...  32.3 us
    pallas_call x1, Pallas kernels, on_device(): pl.pallas_call(factor_kernel, out_shape=(pltpu.VMEM((NB, WIDTH), jnp.floa...  19.7 us
    all_to_all x1, waiting for transfers between devices, on_device(): lax.all_to_all(jnp.broadcast_to(piece[None], (2 * columns, *piece.shape))...  13.1 us
    all_to_all x1, starting transfers between devices, on_device(): lax.all_to_all(matrix.reshape(columns, -1, WIDTH), 'pcol', 0, 0, tiled=True)  10.2 us
    all_to_all x1, waiting for transfers between devices, on_device(): lax.all_to_all(matrix.reshape(columns, -1, WIDTH), 'pcol', 0, 0, tiled=True)  9.6 us
    all_to_all x1, waiting for transfers between devices, on_device(): own = lax.all_to_all(copies, 'pcol', 0, 0, tiled=True)  8.73 us
    all_to_all x1, starting transfers between devices, on_device(): lax.all_to_all(jnp.broadcast_to(piece[None], (2 * columns, *piece.shape))...  5.77 us
    all_to_all x1, starting transfers between devices, on_device(): lax.all_to_all(jnp.concatenate([along, along], axis=0), plane, 0, 0, tile...  4.1 us
  transfers between devices with their start and end apart: 4, of which 3 were waited for; matrix products, arithmetic and copies ran while one was open for 2% of the time, Pallas kernels for 17%

profile of v4, /device:TPU:1, one launch (start us, length us, event | category | flops | bytes accessed | tf_op | source)
XLA Modules:
  0.0 114.4 jit_solution(16377064478260141797)
XLA Ops:
  0.6 10.2 %all-to-all-start = ((f32[16,16,512]{2,1,0:T(8,128)}), f32[16,16,512]{2,1,0:T(8,128)S(1)}, u32[]{:S(2)}, u32[]{:S(2)}) async-start(f32[16,16,512]{2,1,0:T(8,128)} %bitcast.10), calls=%async_computation | async-start | bytes 1048576 | tf_op jit(solution)/shard_map/all_to_all | solution.py:184
  10.8 9.6 %all-to-all-done = f32[16,16,512]{2,1,0:T(8,128)S(1)} async-done(((f32[16,16,512]{2,1,0:T(8,128)}), f32[16,16,512]{2,1,0:T(8,128)S(1)}, u32[]{:S(2)}, u32[]{:S(2)}) %all-to-all-start) | async-done | bytes 524320 | tf_op jit(solution)/shard_map/all_to_all | solution.py:184
  20.4 32.3 %all_gather.3 = f32[16,16,512]{2,1,0:T(8,128)S(1)} all-gather(f32[1,16,512]{2,1,0:T(8,128)S(1)} %get-tuple-element.10), channel_id=1, replica_groups={{0,33,64,97,128,161,192,225,256,289,320,353,384,417,448,481},{1,32,65,9..., dimensions={0}, use_global_device_ids=true | all-gather | bytes 557056 | tf_op jit(solution)/shard_map/all_gather | solution.py:189
  52.7 0.9 broadcast_in_dim.15
  53.6 3.5 %all-to-all-start.3 = ((f32[16,16,512]{2,1,0:T(8,128)}), f32[16,16,512]{2,1,0:T(8,128)S(1)}, u32[]{:S(2)}, u32[]{:S(2)}) async-start(f32[16,16,512]{2,1,0:T(8,128)} %broadcast_in_dim.15), calls=%async_computation.3 | async-start | bytes 1048576 | tf_op jit(solution)/shard_map/all_to_all | solution.py:188
  57.1 8.7 %all-to-all-done.3.own = f32[16,16,512]{2,1,0:T(8,128)S(1)} async-done(((f32[16,16,512]{2,1,0:T(8,128)}), f32[16,16,512]{2,1,0:T(8,128)S(1)}, u32[]{:S(2)}, u32[]{:S(2)}) %all-to-all-start.3) | async-done | bytes 524320 | tf_op jit(solution)/shard_map/all_to_all | solution.py:188
  65.8 1.0 broadcast_in_dim.6
  66.8 5.8 %all-to-all-start.2 = ((f32[32,16,384]{2,1,0:T(8,128)}), f32[32,16,384]{2,1,0:T(8,128)S(1)}, u32[]{:S(2)}, u32[]{:S(2)}) async-start(f32[32,16,384]{2,1,0:T(8,128)} %broadcast_in_dim.6), calls=%async_computation.2 | async-start | bytes 1572864 | tf_op jit(solution)/shard_map/all_to_all | solution.py:207
  72.6 1.1 pad_maximum_fusion
  73.7 13.1 %all-to-all-done.2.gathered = f32[32,16,384]{2,1,0:T(8,128)S(1)} async-done(((f32[32,16,384]{2,1,0:T(8,128)}), f32[32,16,384]{2,1,0:T(8,128)S(1)}, u32[]{:S(2)}, u32[]{:S(2)}) %all-to-all-start.2) | async-done | bytes 786464 | tf_op jit(solution)/shard_map/all_to_all | solution.py:207
  86.8 4.1 %all-to-all-start.1 = ((f32[32,16,512]{2,1,0:T(8,128)}), f32[32,16,512]{2,1,0:T(8,128)S(1)}, u32[]{:S(2)}, u32[]{:S(2)}) async-start(f32[32,16,512]{2,1,0:T(8,128)} %pad_maximum_fusion), calls=%async_computation.1 | async-start | bytes 2097152 | tf_op jit(solution)/shard_map/all_to_all | solution.py:210
  90.9 0.6 pad_add_fusion.place
  91.6 19.7 %factor.1 = (f32[256,512]{1,0:T(8,128)S(1)}, f32[1,512]{1,0:T(1,128)}, f32[16,512]{1,0:T(8,128)}) custom-call(s32[4]{0:T(128)} %pad_add_fusion.place, f32[32,16,384]{2,1,0:T(8,128)S(1)} %all-to-all-done.2.gathered, f32[16,16,512]{2,1,0:T(8,128)S(1)} %all-to-all-done.3.own), custom_call_target="tpu_custom_call" | custom-call | flops 400000000 | bytes 3000000 | tf_op jit(solution)/shard_map/factor/pallas_call | solution.py:213
  111.2 0.0 all-to-all-done.1.across
  111.2 3.1 %apply.1 = f32[256,512]{1,0:T(8,128)} custom-call(s32[4]{0:T(128)} %pad_add_fusion.place, f32[256,512]{1,0:T(8,128)} %matrix.1, f32[32,16,512]{2,1,0:T(8,128)S(1)} %all-to-all-done.1.across, f32[256,512]{1,0:T(8,128)S(1)} %get-tuple-element.6.turned_rows), custom_call_target="tpu_custom_call" | custom-call | flops 200000000 | bytes 3000000 | tf_op jit(solution)/shard_map/apply/pallas_call | solution.py:235
  (5 shorter events, 0.0 us)
Async XLA Ops:
  0.6 19.8 %all-to-all-start = ((f32[16,16,512]{2,1,0:T(8,128)}), f32[16,16,512]{2,1,0:T(8,128)S(1)}, u32[]{:S(2)}, u32[]{:S(2)}) async-start(f32[16,16,512]{2,1,0:T(8,128)} %bitcast.10), calls=%async_computation | async-start | bytes 1048576 | tf_op jit(solution)/shard_map/all_to_all | solution.py:184
  53.6 12.2 %all-to-all-start.3 = ((f32[16,16,512]{2,1,0:T(8,128)}), f32[16,16,512]{2,1,0:T(8,128)S(1)}, u32[]{:S(2)}, u32[]{:S(2)}) async-start(f32[16,16,512]{2,1,0:T(8,128)} %broadcast_in_dim.15), calls=%async_computation.3 | async-start | bytes 1048576 | tf_op jit(solution)/shard_map/all_to_all | solution.py:188
  66.8 20.0 %all-to-all-start.2 = ((f32[32,16,384]{2,1,0:T(8,128)}), f32[32,16,384]{2,1,0:T(8,128)S(1)}, u32[]{:S(2)}, u32[]{:S(2)}) async-start(f32[32,16,384]{2,1,0:T(8,128)} %broadcast_in_dim.6), calls=%async_computation.2 | async-start | bytes 1572864 | tf_op jit(solution)/shard_map/all_to_all | solution.py:207
  86.8 24.4 %all-to-all-start.1 = ((f32[32,16,512]{2,1,0:T(8,128)}), f32[32,16,512]{2,1,0:T(8,128)S(1)}, u32[]{:S(2)}, u32[]{:S(2)}) async-start(f32[32,16,512]{2,1,0:T(8,128)} %pad_maximum_fusion), calls=%async_computation.1 | async-start | bytes 2097152 | tf_op jit(solution)/shard_map/all_to_all | solution.py:210

commit v5 on v4

--- a/solution.py
+++ b/solution.py
@@ -1,3 +1,5 @@
+import functools
+
 import jax
 import jax.numpy as jnp
 from jax import lax
@@ -11,6 +13,7 @@
 WIDTH = NB * PANELS
 BLOCK = 128
 STEP = 8
+NEAR = 2
 PROW = ("z", "yh")
 HIGHEST = lax.Precision.HIGHEST
 
@@ -32,7 +35,7 @@
     return high, middle, rest - middle
 
 
-def factor_block(block, reciprocals_out):
+def factor_block(block, reciprocals_out, between):
     sublane = lax.broadcasted_iota(jnp.int32, (STEP, BLOCK), 0)
     lane = lax.broadcasted_iota(jnp.int32, (STEP, BLOCK), 1)
 
@@ -45,19 +48,23 @@
     pivots = jnp.zeros((STEP, BLOCK), jnp.float32)
     steps = BLOCK // STEP
     columns = None
+    lefts, rights = [], []
     for step in range(steps):
         at = STEP * step
-        ahead = step < steps - 1
+        even = step % 2 == 0
+        near = range(1, min(NEAR + even, steps - 1 - step) + 1)
         current = (lane >= at) & (lane < at + STEP)
         rows = block[at : at + STEP, :]
         if columns is None:
             columns = [spread_column(rows, at + j) for j in range(STEP)]
         rows = jnp.where(current, jnp.where(lane == sublane + at, 1.0, 0.0), rows)
-        if ahead:
-            next_rows = block[at + STEP : at + 2 * STEP, :]
-            below = [spread_column(next_rows, at + j) for j in range(STEP)]
-            upcoming = [spread_column(next_rows, at + STEP + j) for j in range(STEP)]
-            next_rows = jnp.where(current, 0.0, next_rows)
+        next_rows, below, upcoming = {}, {}, []
+        for group in near:
+            next_rows[group] = block[at + STEP * group : at + STEP * (group + 1), :]
+            below[group] = [spread_column(next_rows[group], at + j) for j in range(STEP)]
+            if group == 1:
+                upcoming = [spread_column(next_rows[1], at + STEP + j) for j in range(STEP)]
+            next_rows[group] = jnp.where(current, 0.0, next_rows[group])
         reciprocals = jnp.zeros((STEP, BLOCK), jnp.float32)
         for k in range(STEP):
             pivot = spread_row(columns[k], k)
@@ -67,40 +74,61 @@
                 columns[j] = columns[j] - factor * spread_row(columns[j], k)
             pivot_row = spread_row(rows, k)
             rows = rows - factor * pivot_row
-            if ahead:
-                below_factor = below[k] * reciprocal
-                for j in range(STEP):
-                    upcoming[j] = upcoming[j] - below_factor * spread_row(below[k], j)
+            for group in near:
+                below_factor = below[group][k] * reciprocal
+                if group == 1:
+                    for j in range(STEP):
+                        upcoming[j] = upcoming[j] - below_factor * spread_row(below[1][k], j)
                 for j in range(k + 1, STEP):
-                    below[j] = below[j] - below[k] * spread_row(factor, j)
-                next_rows = next_rows - below_factor * pivot_row
+                    below[group][j] = below[group][j] - below[group][k] * spread_row(factor, j)
+                next_rows[group] = next_rows[group] - below_factor * pivot_row
             reciprocals = jnp.where(sublane == k, reciprocal, reciprocals)
             pivots = jnp.where(lane == at + k, pivot, pivots)
         block[at : at + STEP, :] = rows
         reciprocals_out[at : at + STEP, :] = reciprocals
-        if ahead:
-            block[at + STEP : at + 2 * STEP, :] = next_rows
-            columns = upcoming
-        if step < steps - 2:
-            later = at + 2 * STEP
+        for group in near:
+            block[at + STEP * group : at + STEP * (group + 1), :] = next_rows[group]
+        columns = upcoming
+        later = STEP * (step - step % 2 + 2 + NEAR)
+        if later < BLOCK:
             a, b, c = split(rows * reciprocals)
+            if even:
+                rows = jnp.where((lane >= at + STEP) & (lane < at + 2 * STEP), 0.0, rows)
             d, e, f = split(rows)
-            change = lax.dot_general(
-                jnp.concatenate([a, a, b, b, a, c], axis=0),
-                jnp.concatenate([d, e, d, e, f, d], axis=0),
-                (((0,), (0,)), ((), ())),
-                preferred_element_type=jnp.float32,
-            )
-            lanes = lax.broadcasted_iota(jnp.int32, (BLOCK - later, BLOCK), 1)
-            block[later:, :] = (
-                jnp.where((lanes >= at) & (lanes < at + STEP), 0.0, block[later:, :])
-                - change[later:, :]
-            )
+            lefts += [a, a, b, b, a, c]
+            rights += [d, e, d, e, f, d]
+            if not even:
+                change = lax.dot_general(
+                    jnp.concatenate(lefts, axis=0),
+                    jnp.concatenate(rights, axis=0),
+                    (((0,), (0,)), ((), ())),
+                    preferred_element_type=jnp.float32,
+                )
+                lefts, rights = [], []
+                lanes = lax.broadcasted_iota(jnp.int32, (BLOCK - later, BLOCK), 1)
+                block[later:, :] = (
+                    jnp.where((lanes >= at - STEP) & (lanes < at + STEP), 0.0, block[later:, :])
+                    - change[later:, :]
+                )
+        between()
     return pivots[:1, :]
 
 
 def factor_kernel(
-    place, gathered, own, turned_rows, pivots, panel, corner, work, inverse, factored, block, reciprocals
+    place,
+    gathered,
+    own,
+    turned_rows,
+    pivots,
+    panel,
+    corner,
+    work,
+    inverse,
+    factored,
+    left,
+    ahead,
+    block,
+    reciprocals,
 ):
     row_block, col_block, odd = place[0], place[1], place[2]
     for at in range(0, 2 * 16, 2):
@@ -115,41 +143,91 @@
     work[half : half + quarter, quarter:half] = corner[quarter:half, half:].T
     work[half : half + quarter, :quarter] = corner[half : half + quarter, half:]
     work[half + quarter :, quarter:half] = corner[half + quarter :, half:]
-    inverse[...] = jnp.zeros((WIDTH, WIDTH), jnp.float32)
-    turned_rows[...] = jnp.zeros((NB, WIDTH), jnp.float32)
     lower = lax.broadcasted_iota(jnp.int32, (BLOCK, BLOCK), 0) >= lax.broadcasted_iota(
         jnp.int32, (BLOCK, BLOCK), 1
     )
-    rows = own[...].reshape(NB, WIDTH)
+    queue = []
+
+    def between():
+        if queue:
+            queue.pop(0)()
+
+    def set_columns(at):
+        columns = own[:, :, at : at + BLOCK].reshape(NB, BLOCK)
+        if at > 0:
+            for row in range(0, NB, BLOCK):
+                ahead[row : row + BLOCK, :] = columns[row : row + BLOCK] + product(
+                    own[row // 16 : (row + BLOCK) // 16, :, :at].reshape(BLOCK, at),
+                    inverse[at : at + BLOCK, :at],
+                    1,
+                    1,
+                )
+        else:
+            ahead[...] = columns
+
+    def set_left(base, row, turned):
+        left[row : row + BLOCK, :] = product(
+            work[row : row + BLOCK, base : base + BLOCK], turned, 1, 1
+        )
+
+    def update_work(row, column, block_pivots):
+        work[row : row + BLOCK, column : column + BLOCK] = work[
+            row : row + BLOCK, column : column + BLOCK
+        ] - product(
+            left[row : row + BLOCK, :], left[column : column + BLOCK, :] / block_pivots, 1, 1
+        )
+
+    def update_inverse(base, row, scaled):
+        multipliers = product(left[row : row + BLOCK, :], scaled, 1, 0)
+        inverse[row : row + BLOCK, base : base + BLOCK] = -multipliers
+        if base > 0:
+            inverse[row : row + BLOCK, :base] = inverse[row : row + BLOCK, :base] - product(
+                multipliers, inverse[base : base + BLOCK, :base], 1, 0
+            )
+
+    def set_factored(base, turned):
+        part = product(ahead[...], turned, 1, 1)
+        if base >= NB:
+            part = jnp.where(row_block == 0, 0.0, part)
+        factored[:, base : base + BLOCK] = part
+
+    def set_turned_rows(base, scaled):
+        weighed = product(factored[:, base : base + BLOCK], scaled, 1, 0)
+        turned_rows[:, base : base + BLOCK] = weighed
+
+    def add_turned_rows(base):
+        turned_rows[:, :base] = turned_rows[:, :base] + product(
+            turned_rows[:, base : base + BLOCK], inverse[base : base + BLOCK, :base], 1, 0
+        )
+
+    set_columns(0)
     for base in range(0, WIDTH, BLOCK):
         end = base + BLOCK
         block[...] = work[base:end, base:end]
-        block_pivots = factor_block(block, reciprocals)
+        block_pivots = factor_block(block, reciprocals, between)
+        while queue:
+            between()
         pivots[:, base:end] = block_pivots
         turned = jnp.where(lower, block[...], 0.0)
         scaled = turned * reciprocals[...]
         if end < WIDTH:
-            left = product(work[end:, base:end], turned, 1, 1)
-            weighed = left / block_pivots
-            for at in range(end, WIDTH, BLOCK):
-                work[at:, at : at + BLOCK] = work[at:, at : at + BLOCK] - product(
-                    left[at - end :], weighed[at - end : at - end + BLOCK], 1, 1
-                )
+            set_left(base, end, turned)
+            update_work(end, end, block_pivots)
+        queue.append(functools.partial(set_factored, base, turned))
+        queue.append(functools.partial(set_turned_rows, base, scaled))
         if base > 0:
-            scaled_rows = product(scaled, inverse[base:end, :base], 1, 0)
-            inverse[base:end, :base] = product(turned, inverse[base:end, :base], 1, 0)
-        inverse[base:end, base:end] = turned
+            queue.append(functools.partial(add_turned_rows, base))
         if end < WIDTH:
-            if base > 0:
-                inverse[end:, :base] = inverse[end:, :base] - product(left, scaled_rows, 1, 0)
-            inverse[end:, base:end] = inverse[end:, base:end] - product(left, scaled, 1, 0)
-        part = product(rows[:, :end], inverse[base:end, :end], 1, 1)
-        turned_rows[:, :end] = turned_rows[:, :end] + product(
-            part / block_pivots, inverse[base:end, :end], 1, 0
-        )
-        if base >= NB:
-            part = jnp.where(row_block == 0, 0.0, part)
-        factored[:, base:end] = part
+            queue.append(functools.partial(update_inverse, base, end, scaled))
+        for row in range(end + BLOCK, WIDTH, BLOCK):
+            queue.append(functools.partial(set_left, base, row, turned))
+            for column in range(end, row + BLOCK, BLOCK):
+                queue.append(functools.partial(update_work, row, column, block_pivots))
+            queue.append(functools.partial(update_inverse, base, row, scaled))
+        if end < WIDTH:
+            queue.append(functools.partial(set_columns, end))
+    while queue:
+        between()
     panel[...] = factored[pl.ds(pl.multiple_of(16 * col_block, 16), 16), :]
 
 
@@ -224,6 +302,8 @@
             pltpu.VMEM((WIDTH, WIDTH), jnp.float32),
             pltpu.VMEM((WIDTH, WIDTH), jnp.float32),
             pltpu.VMEM((NB, WIDTH), jnp.float32),
+            pltpu.VMEM((WIDTH, BLOCK), jnp.float32),
+            pltpu.VMEM((NB, BLOCK), jnp.float32),
             pltpu.VMEM((BLOCK, BLOCK), jnp.float32),
             pltpu.VMEM((BLOCK, BLOCK), jnp.float32),
         ],

time: 115 us -> 112 us (0.974)
  Pallas kernels: 22.8 us -> 18.6 us
    pallas_call x1, Pallas kernels: 19.7 us -> 15.5 us  [on_device(): pl.pallas_call(factor_kernel, out_shape=(pltpu.VMEM((NB, WIDTH), jnp.floa...]
  transfers between devices with their start and end apart: 4 -> 4, of which waited for: 3 -> 4; matrix products, arithmetic and copies ran while one was open for 2% -> 2% of each run, Pallas kernels for 17% -> 14%
where the time goes in v5:
time: 112 us; the launch traced here: 111 us
  waiting for transfers between devices  32.5 us (29%)
  blocking collectives  32.3 us (29%)
  starting transfers between devices  23.6 us (21%)
  Pallas kernels  18.6 us (17%)
  local copies, waits for them, and re-layouts  1.84 us (2%)
  other arithmetic  1.73 us (2%)
    all_gather x1, blocking collectives, on_device(): lax.all_gather(scattered, ('z', 'pcol'), axis_index_groups=[[z * columns...  32.3 us
    pallas_call x1, Pallas kernels, on_device(): pl.pallas_call(factor_kernel, out_shape=(pltpu.VMEM((NB, WIDTH), jnp.floa...  15.5 us
    all_to_all x1, waiting for transfers between devices, on_device(): lax.all_to_all(jnp.broadcast_to(piece[None], (2 * columns, *piece.shape))...  13.1 us
    all_to_all x1, starting transfers between devices, on_device(): lax.all_to_all(matrix.reshape(columns, -1, WIDTH), 'pcol', 0, 0, tiled=True)  10.2 us
    all_to_all x1, waiting for transfers between devices, on_device(): lax.all_to_all(matrix.reshape(columns, -1, WIDTH), 'pcol', 0, 0, tiled=True)  9.6 us
    all_to_all x1, waiting for transfers between devices, on_device(): own = lax.all_to_all(copies, 'pcol', 0, 0, tiled=True)  8.73 us
    all_to_all x1, starting transfers between devices, on_device(): lax.all_to_all(jnp.broadcast_to(piece[None], (2 * columns, *piece.shape))...  5.77 us
    all_to_all x1, starting transfers between devices, on_device(): lax.all_to_all(jnp.concatenate([along, along], axis=0), plane, 0, 0, tile...  4.1 us
  transfers between devices with their start and end apart: 4, of which 4 were waited for; matrix products, arithmetic and copies ran while one was open for 2% of the time, Pallas kernels for 14%

profile of v5, /device:TPU:1, one launch (start us, length us, event | category | flops | bytes accessed | tf_op | source)
XLA Modules:
  0.0 111.2 jit_solution(141496705300301965)
XLA Ops:
  0.6 10.2 %all-to-all-start = ((f32[16,16,512]{2,1,0:T(8,128)}), f32[16,16,512]{2,1,0:T(8,128)S(1)}, u32[]{:S(2)}, u32[]{:S(2)}) async-start(f32[16,16,512]{2,1,0:T(8,128)} %bitcast.10), calls=%async_computation | async-start | bytes 1048576 | tf_op jit(solution)/shard_map/all_to_all | solution.py:262
  10.8 9.6 %all-to-all-done = f32[16,16,512]{2,1,0:T(8,128)S(1)} async-done(((f32[16,16,512]{2,1,0:T(8,128)}), f32[16,16,512]{2,1,0:T(8,128)S(1)}, u32[]{:S(2)}, u32[]{:S(2)}) %all-to-all-start) | async-done | bytes 524320 | tf_op jit(solution)/shard_map/all_to_all | solution.py:262
  20.4 32.3 %all_gather.3 = f32[16,16,512]{2,1,0:T(8,128)S(1)} all-gather(f32[1,16,512]{2,1,0:T(8,128)S(1)} %get-tuple-element.10), channel_id=1, replica_groups={{0,33,64,97,128,161,192,225,256,289,320,353,384,417,448,481},{1,32,65,9..., dimensions={0}, use_global_device_ids=true | all-gather | bytes 557056 | tf_op jit(solution)/shard_map/all_gather | solution.py:267
  52.7 0.9 broadcast_in_dim.15
  53.6 3.5 %all-to-all-start.3 = ((f32[16,16,512]{2,1,0:T(8,128)}), f32[16,16,512]{2,1,0:T(8,128)S(1)}, u32[]{:S(2)}, u32[]{:S(2)}) async-start(f32[16,16,512]{2,1,0:T(8,128)} %broadcast_in_dim.15), calls=%async_computation.3 | async-start | bytes 1048576 | tf_op jit(solution)/shard_map/all_to_all | solution.py:266
  57.1 8.7 %all-to-all-done.3.own = f32[16,16,512]{2,1,0:T(8,128)S(1)} async-done(((f32[16,16,512]{2,1,0:T(8,128)}), f32[16,16,512]{2,1,0:T(8,128)S(1)}, u32[]{:S(2)}, u32[]{:S(2)}) %all-to-all-start.3) | async-done | bytes 524320 | tf_op jit(solution)/shard_map/all_to_all | solution.py:266
  65.8 1.0 broadcast_in_dim.6
  66.8 5.8 %all-to-all-start.2 = ((f32[32,16,384]{2,1,0:T(8,128)}), f32[32,16,384]{2,1,0:T(8,128)S(1)}, u32[]{:S(2)}, u32[]{:S(2)}) async-start(f32[32,16,384]{2,1,0:T(8,128)} %broadcast_in_dim.6), calls=%async_computation.2 | async-start | bytes 1572864 | tf_op jit(solution)/shard_map/all_to_all | solution.py:285
  72.6 1.1 pad_maximum_fusion
  73.7 13.1 %all-to-all-done.2.gathered = f32[32,16,384]{2,1,0:T(8,128)S(1)} async-done(((f32[32,16,384]{2,1,0:T(8,128)}), f32[32,16,384]{2,1,0:T(8,128)S(1)}, u32[]{:S(2)}, u32[]{:S(2)}) %all-to-all-start.2) | async-done | bytes 786464 | tf_op jit(solution)/shard_map/all_to_all | solution.py:285
  86.8 4.1 %all-to-all-start.1 = ((f32[32,16,512]{2,1,0:T(8,128)}), f32[32,16,512]{2,1,0:T(8,128)S(1)}, u32[]{:S(2)}, u32[]{:S(2)}) async-start(f32[32,16,512]{2,1,0:T(8,128)} %pad_maximum_fusion), calls=%async_computation.1 | async-start | bytes 2097152 | tf_op jit(solution)/shard_map/all_to_all | solution.py:288
  90.9 0.6 pad_add_fusion.place
  91.6 15.5 %factor.1 = (f32[256,512]{1,0:T(8,128)S(1)}, f32[1,512]{1,0:T(1,128)}, f32[16,512]{1,0:T(8,128)}) custom-call(s32[4]{0:T(128)} %pad_add_fusion.place, f32[32,16,384]{2,1,0:T(8,128)S(1)} %all-to-all-done.2.gathered, f32[16,16,512]{2,1,0:T(8,128)S(1)} %all-to-all-done.3.own), custom_call_target="tpu_custom_call" | custom-call | flops 400000000 | bytes 3000000 | tf_op jit(solution)/shard_map/factor/pallas_call | solution.py:291
  107.0 1.0 all-to-all-done.1.across
  108.1 3.1 %apply.1 = f32[256,512]{1,0:T(8,128)} custom-call(s32[4]{0:T(128)} %pad_add_fusion.place, f32[256,512]{1,0:T(8,128)} %matrix.1, f32[32,16,512]{2,1,0:T(8,128)S(1)} %all-to-all-done.1.across, f32[256,512]{1,0:T(8,128)S(1)} %get-tuple-element.6.turned_rows), custom_call_target="tpu_custom_call" | custom-call | flops 200000000 | bytes 3000000 | tf_op jit(solution)/shard_map/apply/pallas_call | solution.py:315
  (5 shorter events, 0.0 us)
Async XLA Ops:
  0.6 19.8 %all-to-all-start = ((f32[16,16,512]{2,1,0:T(8,128)}), f32[16,16,512]{2,1,0:T(8,128)S(1)}, u32[]{:S(2)}, u32[]{:S(2)}) async-start(f32[16,16,512]{2,1,0:T(8,128)} %bitcast.10), calls=%async_computation | async-start | bytes 1048576 | tf_op jit(solution)/shard_map/all_to_all | solution.py:262
  53.6 12.2 %all-to-all-start.3 = ((f32[16,16,512]{2,1,0:T(8,128)}), f32[16,16,512]{2,1,0:T(8,128)S(1)}, u32[]{:S(2)}, u32[]{:S(2)}) async-start(f32[16,16,512]{2,1,0:T(8,128)} %broadcast_in_dim.15), calls=%async_computation.3 | async-start | bytes 1048576 | tf_op jit(solution)/shard_map/all_to_all | solution.py:266
  66.8 20.0 %all-to-all-start.2 = ((f32[32,16,384]{2,1,0:T(8,128)}), f32[32,16,384]{2,1,0:T(8,128)S(1)}, u32[]{:S(2)}, u32[]{:S(2)}) async-start(f32[32,16,384]{2,1,0:T(8,128)} %broadcast_in_dim.6), calls=%async_computation.2 | async-start | bytes 1572864 | tf_op jit(solution)/shard_map/all_to_all | solution.py:285
  86.8 21.3 %all-to-all-start.1 = ((f32[32,16,512]{2,1,0:T(8,128)}), f32[32,16,512]{2,1,0:T(8,128)S(1)}, u32[]{:S(2)}, u32[]{:S(2)}) async-start(f32[32,16,512]{2,1,0:T(8,128)} %pad_maximum_fusion), calls=%async_computation.1 | async-start | bytes 2097152 | tf_op jit(solution)/shard_map/all_to_all | solution.py:288

commit v6 on v5

--- a/solution.py
+++ b/solution.py
@@ -131,18 +131,31 @@
     reciprocals,
 ):
     row_block, col_block, odd = place[0], place[1], place[2]
+    first = lax.broadcasted_iota(jnp.int32, (8, BLOCK), 1) < 64
     for at in range(0, 2 * 16, 2):
         for side in range(2):
-            corner[16 * (at + side) : 16 * (at + side + 1), :] = gathered[
-                at + jnp.where(odd == 1, 1 - side, side)
-            ]
+            source = at + jnp.where(odd == 1, 1 - side, side)
+            row = 16 * (at + side)
+            corner[row : row + 16, :BLOCK] = gathered[source, :16]
+            corner[row : row + 16, BLOCK:NB] = gathered[source, 16:32]
+            packed = gathered[source, 32:]
+            turned = pltpu.roll(packed, 64, 1)
+            corner[row : row + 8, NB:] = jnp.where(first, packed, turned)
+            corner[row + 8 : row + 16, NB:] = jnp.where(first, turned, packed)
     half, quarter = NB, BLOCK
-    work[:half, :half] = corner[:half, :half]
-    work[half:, half:] = corner[half:, :half]
-    work[half + quarter :, :quarter] = corner[:quarter, half:].T
-    work[half : half + quarter, quarter:half] = corner[quarter:half, half:].T
-    work[half : half + quarter, :quarter] = corner[half : half + quarter, half:]
-    work[half + quarter :, quarter:half] = corner[half + quarter :, half:]
+    same = (lax.broadcasted_iota(jnp.int32, (BLOCK, BLOCK), 0) < 64) == (
+        lax.broadcasted_iota(jnp.int32, (BLOCK, BLOCK), 1) < 64
+    )
+    for at in range(0, WIDTH, BLOCK):
+        work[at : at + BLOCK, at : at + BLOCK] = corner[at : at + BLOCK, :BLOCK]
+    for at in range(0, WIDTH, NB):
+        work[at + BLOCK : at + NB, at : at + BLOCK] = jnp.where(
+            same, corner[at + BLOCK : at + NB, NB:], corner[at : at + BLOCK, NB:].T
+        )
+    work[half + quarter :, :quarter] = corner[:quarter, BLOCK:NB].T
+    work[half : half + quarter, quarter:half] = corner[quarter:half, BLOCK:NB].T
+    work[half : half + quarter, :quarter] = corner[half : half + quarter, BLOCK:NB]
+    work[half + quarter :, quarter:half] = corner[half + quarter :, BLOCK:NB]
     lower = lax.broadcasted_iota(jnp.int32, (BLOCK, BLOCK), 0) >= lax.broadcasted_iota(
         jnp.int32, (BLOCK, BLOCK), 1
     )
@@ -246,16 +259,45 @@
     complement[...] = jnp.where(kept, local[...] - change, 0.0)
 
 
+def pieces_kernel(place, along, pieces):
+    col_block, half = place[1], place[4]
+    lower = jnp.where(col_block >= 8, 1, 0)
+    late = lax.rem(lax.div(col_block, 4), 2)
+
+    def block(index):
+        return along[0, :, pl.ds(pl.multiple_of(index * BLOCK, BLOCK), BLOCK)]
+
+    within = block(2 * half + 1 - lower)
+    other = pltpu.roll(within, 64, 1)
+    first = lax.broadcasted_iota(jnp.int32, (8, BLOCK), 1) < 64
+    packed = jnp.where(
+        lower == late,
+        jnp.where(first, other[:8], within[8:]),
+        jnp.where(first, within[:8], other[8:]),
+    )
+    piece = jnp.concatenate(
+        [
+            block(2 * half + lower),
+            block(jnp.where(half == 0, 3 - lower, lower)),
+            packed,
+        ],
+        axis=0,
+    )
+    pieces[...] = jnp.broadcast_to(piece[None], pieces.shape)
+
+
 def in_vmem(array):
     return pltpu.with_memory_space_constraint(array, pltpu.VMEM)
 
 
 def on_device(matrix):
+    smem = pl.BlockSpec(memory_space=pltpu.SMEM)
+    vmem = pl.BlockSpec(memory_space=pltpu.VMEM)
     half = lax.axis_index("yh")
     row_block = lax.axis_index(PROW)
     col_block = lax.axis_index("pcol")
     depth = lax.axis_index("z")
-    place = jnp.stack([row_block, col_block, depth % 2, (depth + col_block) % 2])
+    place = jnp.stack([row_block, col_block, depth % 2, (depth + col_block) % 2, half])
     place = place.astype(jnp.int32)
     columns = lax.axis_size("pcol")
     plane = ("yh", "pcol")
@@ -273,21 +315,15 @@
             for side in range(2)
         ],
     )
-    corner = along[0]
-    upper = col_block >= columns // 2
-    diagonal = jnp.where(half == 0, corner[:, :NB], corner[:, NB:])
-    mine = jnp.where(
-        half == 0,
-        jnp.where(upper, corner[:, NB : NB + BLOCK], corner[:, NB + BLOCK :]),
-        jnp.where(upper, corner[:, BLOCK:NB], corner[:, :BLOCK]),
-    )
-    piece = jnp.concatenate([diagonal, mine], axis=1)
-    gathered = lax.all_to_all(
-        jnp.broadcast_to(piece[None], (2 * columns, *piece.shape)), plane, 0, 0, tiled=True
-    )
+    pieces = pl.pallas_call(
+        pieces_kernel,
+        out_shape=jax.ShapeDtypeStruct((2 * columns, 40, BLOCK), jnp.float32),
+        in_specs=[smem, vmem],
+        out_specs=vmem,
+        name="pieces",
+    )(place, in_vmem(along))
+    gathered = lax.all_to_all(pieces, plane, 0, 0, tiled=True)
     across = lax.all_to_all(jnp.concatenate([along, along], axis=0), plane, 0, 0, tiled=True)
-    smem = pl.BlockSpec(memory_space=pltpu.SMEM)
-    vmem = pl.BlockSpec(memory_space=pltpu.VMEM)
     turned_rows, pivots, panel = pl.pallas_call(
         factor_kernel,
         out_shape=(

time: 112 us -> 105 us (0.938)
  blocking collectives: 32.3 us -> 51.4 us
  waiting for transfers between devices: 32.5 us -> 13.4 us
  starting transfers between devices: 23.6 us -> 16 us
  Pallas kernels: 18.6 us -> 20.3 us
    all_to_all x0 -> x1, blocking collectives: none -> 19.8 us  [on_device(): lax.all_to_all(matrix.reshape(columns, -1, WIDTH), 'pcol', 0, 0, tiled=True)]
    all_to_all x2 -> x1, waiting for transfers between devices: 22.7 us -> 11.7 us  [on_device(): gathered = lax.all_to_all(pieces, plane, 0, 0, tiled=True)]
    all_to_all x2 -> x1, starting transfers between devices: 16 us -> 7.18 us  [on_device(): gathered = lax.all_to_all(pieces, plane, 0, 0, tiled=True)]
    all_to_all x1, waiting for transfers between devices: 8.73 us -> 0.01 us  [on_device(): own = lax.all_to_all(copies, 'pcol', 0, 0, tiled=True)]
    pallas_call x0 -> x1, Pallas kernels: none -> 1.64 us  [on_device(): pl.pallas_call(pieces_kernel, out_shape=jax.ShapeDtypeStruct((2 * columns...]
    all_to_all x1, starting transfers between devices: 3.47 us -> 4.78 us  [on_device(): own = lax.all_to_all(copies, 'pcol', 0, 0, tiled=True)]
  transfers between devices with their start and end apart: 4 -> 3, of which waited for: 4 -> 2; matrix products, arithmetic and copies ran while one was open for 2% -> 2% of each run, Pallas kernels for 14% -> 16%
where the time goes in v6:
time: 105 us; the launch traced here: 104 us
  blocking collectives  51.4 us (49%)
  Pallas kernels  20.3 us (19%)
  starting transfers between devices  16 us (15%)
  waiting for transfers between devices  13.4 us (13%)
  local copies, waits for them, and re-layouts  1.47 us (1%)
  other arithmetic  1.1 us (1%)
    all_gather x1, blocking collectives, on_device(): lax.all_gather(scattered, ('z', 'pcol'), axis_index_groups=[[z * columns...  31.6 us
    all_to_all x1, blocking collectives, on_device(): lax.all_to_all(matrix.reshape(columns, -1, WIDTH), 'pcol', 0, 0, tiled=True)  19.8 us
    pallas_call x1, Pallas kernels, on_device(): pl.pallas_call(factor_kernel, out_shape=(pltpu.VMEM((NB, WIDTH), jnp.floa...  15.5 us
    all_to_all x1, waiting for transfers between devices, on_device(): gathered = lax.all_to_all(pieces, plane, 0, 0, tiled=True)  11.7 us
    all_to_all x1, starting transfers between devices, on_device(): gathered = lax.all_to_all(pieces, plane, 0, 0, tiled=True)  7.18 us
    all_to_all x1, starting transfers between devices, on_device(): own = lax.all_to_all(copies, 'pcol', 0, 0, tiled=True)  4.78 us
    all_to_all x1, starting transfers between devices, on_device(): lax.all_to_all(jnp.concatenate([along, along], axis=0), plane, 0, 0, tile...  4.07 us
    pallas_call x1, Pallas kernels, on_device(): pl.pallas_call(apply_kernel, out_shape=jax.ShapeDtypeStruct(matrix.shape,...  3.14 us
  transfers between devices with their start and end apart: 3, of which 2 were waited for; matrix products, arithmetic and copies ran while one was open for 2% of the time, Pallas kernels for 16%

profile of v6, /device:TPU:1, one launch (start us, length us, event | category | flops | bytes accessed | tf_op | source)
XLA Modules:
  0.0 104.3 jit_solution(13094999648971501875)
XLA Ops:
  0.6 19.8 %all_to_all.20 = f32[16,16,512]{2,1,0:T(8,128)S(1)} all-to-all(f32[16,16,512]{2,1,0:T(8,128)} %bitcast.9), channel_id=1, replica_groups=mesh['z'=16,'yh'=2,'pcol'=16] {'pcol'}, dimensions={0} | all-to-all | bytes 1048576 | tf_op jit(solution)/shard_map/all_to_all | solution.py:304
  20.4 0.9 broadcast_in_dim.8
  21.3 4.8 %all-to-all-start.3 = ((f32[16,16,512]{2,1,0:T(8,128)}), f32[16,16,512]{2,1,0:T(8,128)S(1)}, u32[]{:S(2)}, u32[]{:S(2)}) async-start(f32[16,16,512]{2,1,0:T(8,128)} %broadcast_in_dim.8), calls=%async_computation.3 | async-start | bytes 1048576 | tf_op jit(solution)/shard_map/all_to_all | solution.py:308
  26.1 0.6 stack.23.place
  26.7 31.6 %all_gather.3.along = f32[16,16,512]{2,1,0:T(8,128)S(1)} all-gather(f32[1,16,512]{2,1,0:T(8,128)S(1)} %get-tuple-element.10), channel_id=1, replica_groups={{0,33,64,97,128,161,192,225,256,289,320,353,384,417,448,481},{1,32,65,9..., dimensions={0}, use_global_device_ids=true | all-gather | bytes 557056 | tf_op jit(solution)/shard_map/all_gather | solution.py:309
  58.3 1.6 %pieces.1 = f32[32,40,128]{2,1,0:T(8,128)} custom-call(s32[5]{0:T(128)} %stack.23.place, f32[16,16,512]{2,1,0:T(8,128)S(1)} %all_gather.3.along), custom_call_target="tpu_custom_call" | custom-call | tf_op jit(solution)/shard_map/pieces/pallas_call | solution.py:318
  59.9 0.0 all-to-all-done.3.own
  59.9 7.2 %all-to-all-start.2 = ((f32[32,40,128]{2,1,0:T(8,128)}), f32[32,40,128]{2,1,0:T(8,128)S(1)}, u32[]{:S(2)}, u32[]{:S(2)}) async-start(f32[32,40,128]{2,1,0:T(8,128)} %pieces.1), calls=%async_computation.2 | async-start | bytes 1310720 | tf_op jit(solution)/shard_map/all_to_all | solution.py:325
  67.1 1.1 %pad_maximum_fusion = f32[32,16,512]{2,1,0:T(8,128)} fusion(f32[16,16,512]{2,1,0:T(8,128)S(1)} %all_gather.3.along), kind=kLoop, calls=%fused_computation | loop fusion | flops 262144 | bytes 1572864 | tf_op jit(solution)/shard_map/concatenate | solution.py:326
  68.2 11.7 %all-to-all-done.2.gathered = f32[32,40,128]{2,1,0:T(8,128)S(1)} async-done(((f32[32,40,128]{2,1,0:T(8,128)}), f32[32,40,128]{2,1,0:T(8,128)S(1)}, u32[]{:S(2)}, u32[]{:S(2)}) %all-to-all-start.2) | async-done | bytes 655392 | tf_op jit(solution)/shard_map/all_to_all | solution.py:325
  80.0 4.1 %all-to-all-start.1 = ((f32[32,16,512]{2,1,0:T(8,128)}), f32[32,16,512]{2,1,0:T(8,128)S(1)}, u32[]{:S(2)}, u32[]{:S(2)}) async-start(f32[32,16,512]{2,1,0:T(8,128)} %pad_maximum_fusion), calls=%async_computation.1 | async-start | bytes 2097152 | tf_op jit(solution)/shard_map/all_to_all | solution.py:326
  84.0 15.5 %factor.1 = (f32[256,512]{1,0:T(8,128)S(1)}, f32[1,512]{1,0:T(1,128)}, f32[16,512]{1,0:T(8,128)}) custom-call(s32[5]{0:T(128)} %stack.23.place, f32[32,40,128]{2,1,0:T(8,128)S(1)} %all-to-all-done.2.gathered, f32[16,16,512]{2,1,0:T(8,128)S(1)} %all-to-all-done.3.own), custom_call_target="tpu_custom_call" | custom-call | flops 400000000 | bytes 3000000 | tf_op jit(solution)/shard_map/factor/pallas_call | solution.py:327
  99.5 1.7 %all-to-all-done.1.across = f32[32,16,512]{2,1,0:T(8,128)S(1)} async-done(((f32[32,16,512]{2,1,0:T(8,128)}), f32[32,16,512]{2,1,0:T(8,128)S(1)}, u32[]{:S(2)}, u32[]{:S(2)}) %all-to-all-start.1) | async-done | bytes 1048608 | tf_op jit(solution)/shard_map/all_to_all | solution.py:326
  101.2 3.1 %apply.1 = f32[256,512]{1,0:T(8,128)} custom-call(s32[5]{0:T(128)} %stack.23.place, f32[256,512]{1,0:T(8,128)} %matrix.1, f32[32,16,512]{2,1,0:T(8,128)S(1)} %all-to-all-done.1.across, f32[256,512]{1,0:T(8,128)S(1)} %get-tuple-element.6.turned_rows), custom_call_target="tpu_custom_call" | custom-call | flops 200000000 | bytes 3000000 | tf_op jit(solution)/shard_map/apply/pallas_call | solution.py:351
  (1 shorter events, 0.0 us)
Async XLA Ops:
  21.3 38.7 %all-to-all-start.3 = ((f32[16,16,512]{2,1,0:T(8,128)}), f32[16,16,512]{2,1,0:T(8,128)S(1)}, u32[]{:S(2)}, u32[]{:S(2)}) async-start(f32[16,16,512]{2,1,0:T(8,128)} %broadcast_in_dim.8), calls=%async_computation.3 | async-start | bytes 1048576 | tf_op jit(solution)/shard_map/all_to_all | solution.py:308
  59.9 20.0 %all-to-all-start.2 = ((f32[32,40,128]{2,1,0:T(8,128)}), f32[32,40,128]{2,1,0:T(8,128)S(1)}, u32[]{:S(2)}, u32[]{:S(2)}) async-start(f32[32,40,128]{2,1,0:T(8,128)} %pieces.1), calls=%async_computation.2 | async-start | bytes 1310720 | tf_op jit(solution)/shard_map/all_to_all | solution.py:325
  80.0 21.2 %all-to-all-start.1 = ((f32[32,16,512]{2,1,0:T(8,128)}), f32[32,16,512]{2,1,0:T(8,128)S(1)}, u32[]{:S(2)}, u32[]{:S(2)}) async-start(f32[32,16,512]{2,1,0:T(8,128)} %pad_maximum_fusion), calls=%async_computation.1 | async-start | bytes 2097152 | tf_op jit(solution)/shard_map/all_to_all | solution.py:326

commit v7 on v6

--- a/solution.py
+++ b/solution.py
@@ -259,7 +259,7 @@
     complement[...] = jnp.where(kept, local[...] - change, 0.0)
 
 
-def pieces_kernel(place, along, pieces):
+def pieces_kernel(place, along, pieces, piece, sent):
     col_block, half = place[1], place[4]
     lower = jnp.where(col_block >= 8, 1, 0)
     late = lax.rem(lax.div(col_block, 4), 2)
@@ -275,15 +275,24 @@
         jnp.where(first, other[:8], within[8:]),
         jnp.where(first, within[:8], other[8:]),
     )
-    piece = jnp.concatenate(
-        [
-            block(2 * half + lower),
-            block(jnp.where(half == 0, 3 - lower, lower)),
-            packed,
-        ],
-        axis=0,
-    )
-    pieces[...] = jnp.broadcast_to(piece[None], pieces.shape)
+    piece[:16, :] = block(2 * half + lower)
+    piece[16:32, :] = block(jnp.where(half == 0, 3 - lower, lower))
+    piece[32:, :] = packed
+    spread(piece, pieces, sent)
+
+
+def spread(source, target, sent):
+    copies = [
+        pltpu.make_async_copy(source, target.at[at], sent.at[at]) for at in range(target.shape[0])
+    ]
+    for copy in copies:
+        copy.start()
+    for copy in copies:
+        copy.wait()
+
+
+def copies_kernel(rows, copies, sent):
+    spread(rows.at[0], copies, sent)
 
 
 def in_vmem(array):
@@ -303,8 +312,17 @@
     plane = ("yh", "pcol")
     scattered = lax.all_to_all(
         matrix.reshape(columns, -1, WIDTH), "pcol", 0, 0, tiled=True
-    )[0]
-    copies = jnp.broadcast_to(scattered[None], (columns, *scattered.shape))
+    )
+    copies = pl.pallas_call(
+        copies_kernel,
+        out_shape=jax.ShapeDtypeStruct(scattered.shape, jnp.float32),
+        in_specs=[vmem],
+        out_specs=pl.BlockSpec(memory_space=pl.ANY),
+        scratch_shapes=[pltpu.SemaphoreType.DMA((columns,))],
+        compiler_params=pltpu.CompilerParams(vmem_limit_bytes=4 << 20),
+        name="copies",
+    )(in_vmem(scattered))
+    scattered = scattered[0]
     own = lax.all_to_all(copies, "pcol", 0, 0, tiled=True)
     along = lax.all_gather(
         scattered,
@@ -319,7 +337,12 @@
         pieces_kernel,
         out_shape=jax.ShapeDtypeStruct((2 * columns, 40, BLOCK), jnp.float32),
         in_specs=[smem, vmem],
-        out_specs=vmem,
+        out_specs=pl.BlockSpec(memory_space=pl.ANY),
+        scratch_shapes=[
+            pltpu.VMEM((40, BLOCK), jnp.float32),
+            pltpu.SemaphoreType.DMA((2 * columns,)),
+        ],
+        compiler_params=pltpu.CompilerParams(vmem_limit_bytes=4 << 20),
         name="pieces",
     )(place, in_vmem(along))
     gathered = lax.all_to_all(pieces, plane, 0, 0, tiled=True)

time: 105 us -> 105 us (level)
  local copies, waits for them, and re-layouts: 1.47 us -> 0.09 us
  transfers between devices with their start and end apart: 3 -> 3, of which waited for: 2 -> 2; matrix products, arithmetic and copies ran while one was open for 2% -> 1% of each run, Pallas kernels for 16% -> 17%
where the time goes in v7:
time: 105 us; the launch traced here: 104 us
  blocking collectives  51.4 us (49%)
  Pallas kernels  21.3 us (20%)
  starting transfers between devices  16.1 us (15%)
  waiting for transfers between devices  13.4 us (13%)
  other arithmetic  1.1 us (1%)
    all_gather x1, blocking collectives, on_device(): lax.all_gather(scattered, ('z', 'pcol'), axis_index_groups=[[z * columns...  31.6 us
    all_to_all x1, blocking collectives, on_device(): lax.all_to_all(matrix.reshape(columns, -1, WIDTH), 'pcol', 0, 0, tiled=True)  19.8 us
    pallas_call x1, Pallas kernels, on_device(): pl.pallas_call(factor_kernel, out_shape=(pltpu.VMEM((NB, WIDTH), jnp.floa...  15.5 us
    all_to_all x1, waiting for transfers between devices, on_device(): gathered = lax.all_to_all(pieces, plane, 0, 0, tiled=True)  11.7 us
    all_to_all x1, starting transfers between devices, on_device(): gathered = lax.all_to_all(pieces, plane, 0, 0, tiled=True)  7.28 us
    all_to_all x1, starting transfers between devices, on_device(): own = lax.all_to_all(copies, 'pcol', 0, 0, tiled=True)  4.79 us
    all_to_all x1, starting transfers between devices, on_device(): lax.all_to_all(jnp.concatenate([along, along], axis=0), plane, 0, 0, tile...  4.07 us
    pallas_call x1, Pallas kernels, on_device(): pl.pallas_call(apply_kernel, out_shape=jax.ShapeDtypeStruct(matrix.shape,...  3.15 us
  transfers between devices with their start and end apart: 3, of which 2 were waited for; matrix products, arithmetic and copies ran while one was open for 1% of the time, Pallas kernels for 17%

profile of v7, /device:TPU:1, one launch (start us, length us, event | category | flops | bytes accessed | tf_op | source)
XLA Modules:
  0.0 104.2 jit_solution(5712166877511798786)
XLA Ops:
  0.6 19.8 %all_to_all.20.rows = f32[16,16,512]{2,1,0:T(8,128)S(1)} all-to-all(f32[16,16,512]{2,1,0:T(8,128)} %bitcast.7), channel_id=1, replica_groups=mesh['z'=16,'yh'=2,'pcol'=16] {'pcol'}, dimensions={0} | all-to-all | bytes 1048576 | tf_op jit(solution)/shard_map/all_to_all | solution.py:313
  20.4 0.9 copies.1
  21.3 4.8 %all-to-all-start.3 = ((f32[16,16,512]{2,1,0:T(8,128)}), f32[16,16,512]{2,1,0:T(8,128)S(1)}, u32[]{:S(2)}, u32[]{:S(2)}) async-start(f32[16,16,512]{2,1,0:T(8,128)} %copies.1), calls=%async_computation.3 | async-start | bytes 1048576 | tf_op jit(solution)/shard_map/all_to_all | solution.py:326
  26.1 0.1 stack.23.place
  26.2 0.0 copy-start
  26.2 31.6 %all_gather.3.along = f32[16,16,512]{2,1,0:T(8,128)S(1)} all-gather(f32[1,16,512]{2,1,0:T(8,128)S(1)} %slice.4), channel_id=1, replica_groups={{0,33,64,97,128,161,192,225,256,289,320,353,384,417,448,481},{1,32,65,9..., dimensions={0}, use_global_device_ids=true | all-gather | bytes 557056 | tf_op jit(solution)/shard_map/all_gather | solution.py:327
  57.9 0.0 copy-done
  57.9 1.8 %pieces.1 = f32[32,40,128]{2,1,0:T(8,128)} custom-call(s32[5]{0:T(128)S(1)} %stack.23.place, f32[16,16,512]{2,1,0:T(8,128)S(1)} %all_gather.3.along), custom_call_target="tpu_custom_call" | custom-call | tf_op jit(solution)/shard_map/pieces/pallas_call | solution.py:336
  59.7 0.0 all-to-all-done.3.own
  59.7 7.3 %all-to-all-start.2 = ((f32[32,40,128]{2,1,0:T(8,128)}), f32[32,40,128]{2,1,0:T(8,128)S(1)}, u32[]{:S(2)}, u32[]{:S(2)}) async-start(f32[32,40,128]{2,1,0:T(8,128)} %pieces.1), calls=%async_computation.2 | async-start | bytes 1310720 | tf_op jit(solution)/shard_map/all_to_all | solution.py:348
  67.0 1.1 %pad_maximum_fusion = f32[32,16,512]{2,1,0:T(8,128)} fusion(f32[16,16,512]{2,1,0:T(8,128)S(1)} %all_gather.3.along), kind=kLoop, calls=%fused_computation | loop fusion | flops 262144 | bytes 1572864 | tf_op jit(solution)/shard_map/concatenate | solution.py:349
  68.1 11.7 %all-to-all-done.2.gathered = f32[32,40,128]{2,1,0:T(8,128)S(1)} async-done(((f32[32,40,128]{2,1,0:T(8,128)}), f32[32,40,128]{2,1,0:T(8,128)S(1)}, u32[]{:S(2)}, u32[]{:S(2)}) %all-to-all-start.2) | async-done | bytes 655392 | tf_op jit(solution)/shard_map/all_to_all | solution.py:348
  79.8 4.1 %all-to-all-start.1 = ((f32[32,16,512]{2,1,0:T(8,128)}), f32[32,16,512]{2,1,0:T(8,128)S(1)}, u32[]{:S(2)}, u32[]{:S(2)}) async-start(f32[32,16,512]{2,1,0:T(8,128)} %pad_maximum_fusion), calls=%async_computation.1 | async-start | bytes 2097152 | tf_op jit(solution)/shard_map/all_to_all | solution.py:349
  83.9 15.5 %factor.1 = (f32[256,512]{1,0:T(8,128)S(1)}, f32[1,512]{1,0:T(1,128)}, f32[16,512]{1,0:T(8,128)}) custom-call(s32[5]{0:T(128)} %copy-done, f32[32,40,128]{2,1,0:T(8,128)S(1)} %all-to-all-done.2.gathered, f32[16,16,512]{2,1,0:T(8,128)S(1)} %all-to-all-done.3.own), custom_call_target="tpu_custom_call" | custom-call | flops 400000000 | bytes 3000000 | tf_op jit(solution)/shard_map/factor/pallas_call | solution.py:350
  99.4 1.7 %all-to-all-done.1.across = f32[32,16,512]{2,1,0:T(8,128)S(1)} async-done(((f32[32,16,512]{2,1,0:T(8,128)}), f32[32,16,512]{2,1,0:T(8,128)S(1)}, u32[]{:S(2)}, u32[]{:S(2)}) %all-to-all-start.1) | async-done | bytes 1048608 | tf_op jit(solution)/shard_map/all_to_all | solution.py:349
  101.0 3.1 %apply.1 = f32[256,512]{1,0:T(8,128)} custom-call(s32[5]{0:T(128)} %copy-done, f32[256,512]{1,0:T(8,128)} %matrix.1, f32[32,16,512]{2,1,0:T(8,128)S(1)} %all-to-all-done.1.across, f32[256,512]{1,0:T(8,128)S(1)} %get-tuple-element.6.turned_rows), custom_call_target="tpu_custom_call" | custom-call | flops 200000000 | bytes 3000000 | tf_op jit(solution)/shard_map/apply/pallas_call | solution.py:374
  (1 shorter events, 0.0 us)
Async XLA Ops:
  21.3 38.3 %all-to-all-start.3 = ((f32[16,16,512]{2,1,0:T(8,128)}), f32[16,16,512]{2,1,0:T(8,128)S(1)}, u32[]{:S(2)}, u32[]{:S(2)}) async-start(f32[16,16,512]{2,1,0:T(8,128)} %copies.1), calls=%async_computation.3 | async-start | bytes 1048576 | tf_op jit(solution)/shard_map/all_to_all | solution.py:326
  26.2 31.7 %copy-start = (s32[5]{0:T(128)}, s32[5]{0:T(128)S(1)}, u32[]{:S(2)}) copy-start(s32[5]{0:T(128)S(1)} %stack.23.place) | copy-start | bytes 64
  59.7 20.1 %all-to-all-start.2 = ((f32[32,40,128]{2,1,0:T(8,128)}), f32[32,40,128]{2,1,0:T(8,128)S(1)}, u32[]{:S(2)}, u32[]{:S(2)}) async-start(f32[32,40,128]{2,1,0:T(8,128)} %pieces.1), calls=%async_computation.2 | async-start | bytes 1310720 | tf_op jit(solution)/shard_map/all_to_all | solution.py:348
  79.8 21.2 %all-to-all-start.1 = ((f32[32,16,512]{2,1,0:T(8,128)}), f32[32,16,512]{2,1,0:T(8,128)S(1)}, u32[]{:S(2)}, u32[]{:S(2)}) async-start(f32[32,16,512]{2,1,0:T(8,128)} %pad_maximum_fusion), calls=%async_computation.1 | async-start | bytes 2097152 | tf_op jit(solution)/shard_map/all_to_all | solution.py:349

commit v8 on v6

--- a/solution.py
+++ b/solution.py
@@ -283,7 +283,7 @@
         ],
         axis=0,
     )
-    pieces[...] = jnp.broadcast_to(piece[None], pieces.shape)
+    pieces[...] = piece
 
 
 def in_vmem(array):
@@ -317,11 +317,13 @@
     )
     pieces = pl.pallas_call(
         pieces_kernel,
-        out_shape=jax.ShapeDtypeStruct((2 * columns, 40, BLOCK), jnp.float32),
+        out_shape=jax.ShapeDtypeStruct((40, BLOCK), jnp.float32),
         in_specs=[smem, vmem],
         out_specs=vmem,
+        compiler_params=pltpu.CompilerParams(vmem_limit_bytes=4 << 20),
         name="pieces",
     )(place, in_vmem(along))
+    pieces = jnp.broadcast_to(pieces[None], (2 * columns, *pieces.shape))
     gathered = lax.all_to_all(pieces, plane, 0, 0, tiled=True)
     across = lax.all_to_all(jnp.concatenate([along, along], axis=0), plane, 0, 0, tiled=True)
     turned_rows, pivots, panel = pl.pallas_call(

time: 105 us -> 104 us (level)
  Pallas kernels: 20.3 us -> 19.2 us
  transfers between devices with their start and end apart: 3 -> 3, of which waited for: 2 -> 2; matrix products, arithmetic and copies ran while one was open for 2% -> 1% of each run, Pallas kernels for 16% -> 16%
where the time goes in v8:
time: 104 us
  blocking collectives  51.4 us (49%)
  Pallas kernels  19.2 us (18%)
  starting transfers between devices  16.1 us (15%)
  waiting for transfers between devices  13.4 us (13%)
  local copies, waits for them, and re-layouts  1.87 us (2%)
  other arithmetic  1.1 us (1%)
    all_gather x1, blocking collectives, on_device(): lax.all_gather(scattered, ('z', 'pcol'), axis_index_groups=[[z * columns...  31.6 us
    all_to_all x1, blocking collectives, on_device(): lax.all_to_all(matrix.reshape(columns, -1, WIDTH), 'pcol', 0, 0, tiled=True)  19.8 us
    pallas_call x1, Pallas kernels, on_device(): pl.pallas_call(factor_kernel, out_shape=(pltpu.VMEM((NB, WIDTH), jnp.floa...  15.5 us
    all_to_all x1, waiting for transfers between devices, on_device(): gathered = lax.all_to_all(pieces, plane, 0, 0, tiled=True)  11.7 us
    all_to_all x1, starting transfers between devices, on_device(): gathered = lax.all_to_all(pieces, plane, 0, 0, tiled=True)  7.27 us
    all_to_all x1, starting transfers between devices, on_device(): own = lax.all_to_all(copies, 'pcol', 0, 0, tiled=True)  4.78 us
    all_to_all x1, starting transfers between devices, on_device(): lax.all_to_all(jnp.concatenate([along, along], axis=0), plane, 0, 0, tile...  4.07 us
    pallas_call x1, Pallas kernels, on_device(): pl.pallas_call(apply_kernel, out_shape=jax.ShapeDtypeStruct(matrix.shape,...  3.15 us
  transfers between devices with their start and end apart: 3, of which 2 were waited for; matrix products, arithmetic and copies ran while one was open for 1% of the time, Pallas kernels for 16%

profile of v8, /device:TPU:1, one launch (start us, length us, event | category | flops | bytes accessed | tf_op | source)
XLA Modules:
  0.0 103.8 jit_solution(8966506470329595893)
XLA Ops:
  0.6 19.8 %all_to_all.20 = f32[16,16,512]{2,1,0:T(8,128)S(1)} all-to-all(f32[16,16,512]{2,1,0:T(8,128)} %bitcast.9), channel_id=1, replica_groups=mesh['z'=16,'yh'=2,'pcol'=16] {'pcol'}, dimensions={0} | all-to-all | bytes 1048576 | tf_op jit(solution)/shard_map/all_to_all | solution.py:304
  20.4 0.9 broadcast_in_dim.15
  21.3 4.8 %all-to-all-start.3 = ((f32[16,16,512]{2,1,0:T(8,128)}), f32[16,16,512]{2,1,0:T(8,128)S(1)}, u32[]{:S(2)}, u32[]{:S(2)}) async-start(f32[16,16,512]{2,1,0:T(8,128)} %broadcast_in_dim.15), calls=%async_computation.3 | async-start | bytes 1048576 | tf_op jit(solution)/shard_map/all_to_all | solution.py:308
  26.1 0.1 stack.23.place
  26.1 0.0 copy-start
  26.1 31.6 %all_gather.3.along = f32[16,16,512]{2,1,0:T(8,128)S(1)} all-gather(f32[1,16,512]{2,1,0:T(8,128)S(1)} %get-tuple-element.10), channel_id=1, replica_groups={{0,33,64,97,128,161,192,225,256,289,320,353,384,417,448,481},{1,32,65,9..., dimensions={0}, use_global_device_ids=true | all-gather | bytes 557056 | tf_op jit(solution)/shard_map/all_gather | solution.py:309
  57.8 0.0 copy-done
  57.8 0.6 pieces.1
  58.4 0.0 all-to-all-done.3.own
  58.4 0.9 broadcast_in_dim.6
  59.3 7.3 %all-to-all-start.2 = ((f32[32,40,128]{2,1,0:T(8,128)}), f32[32,40,128]{2,1,0:T(8,128)S(1)}, u32[]{:S(2)}, u32[]{:S(2)}) async-start(f32[32,40,128]{2,1,0:T(8,128)} %broadcast_in_dim.6), calls=%async_computation.2 | async-start | bytes 1310720 | tf_op jit(solution)/shard_map/all_to_all | solution.py:327
  66.6 1.1 %pad_maximum_fusion = f32[32,16,512]{2,1,0:T(8,128)} fusion(f32[16,16,512]{2,1,0:T(8,128)S(1)} %all_gather.3.along), kind=kLoop, calls=%fused_computation | loop fusion | flops 262144 | bytes 1572864 | tf_op jit(solution)/shard_map/concatenate | solution.py:328
  67.7 11.7 %all-to-all-done.2.gathered = f32[32,40,128]{2,1,0:T(8,128)S(1)} async-done(((f32[32,40,128]{2,1,0:T(8,128)}), f32[32,40,128]{2,1,0:T(8,128)S(1)}, u32[]{:S(2)}, u32[]{:S(2)}) %all-to-all-start.2) | async-done | bytes 655392 | tf_op jit(solution)/shard_map/all_to_all | solution.py:327
  79.5 4.1 %all-to-all-start.1 = ((f32[32,16,512]{2,1,0:T(8,128)}), f32[32,16,512]{2,1,0:T(8,128)S(1)}, u32[]{:S(2)}, u32[]{:S(2)}) async-start(f32[32,16,512]{2,1,0:T(8,128)} %pad_maximum_fusion), calls=%async_computation.1 | async-start | bytes 2097152 | tf_op jit(solution)/shard_map/all_to_all | solution.py:328
  83.5 15.5 %factor.1 = (f32[256,512]{1,0:T(8,128)S(1)}, f32[1,512]{1,0:T(1,128)}, f32[16,512]{1,0:T(8,128)}) custom-call(s32[5]{0:T(128)} %copy-done, f32[32,40,128]{2,1,0:T(8,128)S(1)} %all-to-all-done.2.gathered, f32[16,16,512]{2,1,0:T(8,128)S(1)} %all-to-all-done.3.own), custom_call_target="tpu_custom_call" | custom-call | flops 400000000 | bytes 3000000 | tf_op jit(solution)/shard_map/factor/pallas_call | solution.py:329
  99.0 1.7 %all-to-all-done.1.across = f32[32,16,512]{2,1,0:T(8,128)S(1)} async-done(((f32[32,16,512]{2,1,0:T(8,128)}), f32[32,16,512]{2,1,0:T(8,128)S(1)}, u32[]{:S(2)}, u32[]{:S(2)}) %all-to-all-start.1) | async-done | bytes 1048608 | tf_op jit(solution)/shard_map/all_to_all | solution.py:328
  100.7 3.1 %apply.1 = f32[256,512]{1,0:T(8,128)} custom-call(s32[5]{0:T(128)} %copy-done, f32[256,512]{1,0:T(8,128)} %matrix.1, f32[32,16,512]{2,1,0:T(8,128)S(1)} %all-to-all-done.1.across, f32[256,512]{1,0:T(8,128)S(1)} %get-tuple-element.6.turned_rows), custom_call_target="tpu_custom_call" | custom-call | flops 200000000 | bytes 3000000 | tf_op jit(solution)/shard_map/apply/pallas_call | solution.py:353
  (1 shorter events, 0.0 us)
Async XLA Ops:
  21.3 37.1 %all-to-all-start.3 = ((f32[16,16,512]{2,1,0:T(8,128)}), f32[16,16,512]{2,1,0:T(8,128)S(1)}, u32[]{:S(2)}, u32[]{:S(2)}) async-start(f32[16,16,512]{2,1,0:T(8,128)} %broadcast_in_dim.15), calls=%async_computation.3 | async-start | bytes 1048576 | tf_op jit(solution)/shard_map/all_to_all | solution.py:308
  26.1 31.6 %copy-start = (s32[5]{0:T(128)}, s32[5]{0:T(128)S(1)}, u32[]{:S(2)}) copy-start(s32[5]{0:T(128)S(1)} %stack.23.place) | copy-start | bytes 64
  59.3 20.1 %all-to-all-start.2 = ((f32[32,40,128]{2,1,0:T(8,128)}), f32[32,40,128]{2,1,0:T(8,128)S(1)}, u32[]{:S(2)}, u32[]{:S(2)}) async-start(f32[32,40,128]{2,1,0:T(8,128)} %broadcast_in_dim.6), calls=%async_computation.2 | async-start | bytes 1310720 | tf_op jit(solution)/shard_map/all_to_all | solution.py:327
  79.5 21.2 %all-to-all-start.1 = ((f32[32,16,512]{2,1,0:T(8,128)}), f32[32,16,512]{2,1,0:T(8,128)S(1)}, u32[]{:S(2)}, u32[]{:S(2)}) async-start(f32[32,16,512]{2,1,0:T(8,128)} %pad_maximum_fusion), calls=%async_computation.1 | async-start | bytes 2097152 | tf_op jit(solution)/shard_map/all_to_all | solution.py:328
